TPU v7x, 32 devices: a whole 2x2x4 slice. The times are simulated.
32 devices in a mesh: section: 2 (over core), dp: 8 (over z, x), seq: 2 (over y).
Axes of the slice: x: 2, y: 2, z: 4, core: 2. Of those that a mesh axis runs over, the one named last changes fastest.
Arguments:
- image_in: bfloat16 [2, 8, 128, 1536], P(None, 'dp', 'seq'), may hold values from -6 to 6
- text_in: bfloat16 [2, 8, 64, 1536], P(None, 'dp', 'seq'), may hold values from -6 to 6
- image_cot: bfloat16 [2, 8, 128, 1536], P(None, 'dp', 'seq'), may hold values from -6 to 6
- text_cot: bfloat16 [2, 8, 64, 1536], P(None, 'dp', 'seq'), may hold values from -6 to 6
- cond_table: bfloat16 [16, 1536], replicated, may hold values from -6 to 6
- seq_table: int32 [8, 2], replicated, may hold values from 0 to 15, as said below
- text_count: int32 [2, 8, 2], P(None, 'dp'), may hold values from 1 to 32, as said below
- mod_weight: bfloat16 [2, 2, 1536, 9216], P('section', None, 'dp'), may hold values from -0.15625 to 0.15625
- mod_bias: bfloat16 [2, 2, 9216], P('section', None, 'dp'), may hold values from -3 to 3
- qkv_weight: bfloat16 [2, 2, 1536, 4608], P('section', None, 'dp'), may hold values from -0.15625 to 0.15625
- qkv_bias: bfloat16 [2, 2, 4608], P('section', None, 'dp'), may hold values from -1.1953125 to 1.1953125
- qk_gain: bfloat16 [2, 2, 128], P('section', None, 'dp'), may hold values from 0.5 to 1.5
- out_weight: bfloat16 [2, 2, 1536, 1536], P('section', None, 'dp'), may hold values from -1 to 1
- out_bias: bfloat16 [2, 2, 1536], P('section', None, 'dp'), may hold values from -1.796875 to 1.796875
- up_weight: bfloat16 [2, 2, 1536, 6144], P('section', None, 'dp'), may hold values from -0.15625 to 0.15625
- up_bias: bfloat16 [2, 2, 6144], P('section', None, 'dp'), may hold values from -1.796875 to 1.796875
- down_weight: bfloat16 [2, 2, 6144, 1536], P('section', None, 'dp'), may hold values from -0.078125 to 0.078125
- down_bias: bfloat16 [2, 2, 1536], P('section', None, 'dp'), may hold values from -1.796875 to 1.796875
Outputs:
- image_out: bfloat16 [2, 2, 8, 128, 1536], P('section', None, 'dp', 'seq')
- text_out: bfloat16 [2, 2, 8, 64, 1536], P('section', None, 'dp', 'seq')
- image_grad: float32 [2, 2, 8, 128, 1536], P('section', None, 'dp', 'seq')
- text_grad: float32 [2, 2, 8, 64, 1536], P('section', None, 'dp', 'seq')
- modw_grad: float32 [2, 2, 1536, 9216], P('section', None, 'dp')
- modb_grad: float32 [2, 2, 9216], P('section', None, 'dp')
- qkvw_grad: float32 [2, 2, 1536, 4608], P('section', None, 'dp')
- qkvb_grad: float32 [2, 2, 4608], P('section', None, 'dp')
- gain_grad: float32 [2, 2, 128], P('section', None, 'dp')
- outw_grad: float32 [2, 2, 1536, 1536], P('section', None, 'dp')
- outb_grad: float32 [2, 2, 1536], P('section', None, 'dp')
- upw_grad: float32 [2, 2, 1536, 6144], P('section', None, 'dp')
- upb_grad: float32 [2, 2, 6144], P('section', None, 'dp')
- downw_grad: float32 [2, 2, 6144, 1536], P('section', None, 'dp')
- downb_grad: float32 [2, 2, 1536], P('section', None, 'dp')
Inputs may be any that keep to these rules, and one draw needn't show every extreme that they name: `seq_table`: each of the 16 sequence numbers stands exactly once. `text_count`: live text rows held by each device of its sequence; some device holds 32 and some holds 1.
All inputs are finite; a program needn't handle non-finite values.
Results may differ from a plain program's by a relative error of at most 0.04.
Values may be sent and summed in bfloat16 or wider, within the bound.
A program may use at most 576 MiB of HBM per device.

v0:
```python
import jax
import jax.numpy as jnp
from jax import lax
from jax.sharding import PartitionSpec as P

HEADS = 24
HD = 64


eps_norm = 1e-06
gelu_coef = 0.7978845608028654


def passed_along(value, axis, steps):
    count = lax.axis_size(axis)
    first, last = (max(0, -steps), min(count, count - steps))
    return lax.ppermute(value, axis, [(source, source + steps) for source in range(first, last)])


def layer_norm(values):
    center = values - jnp.mean(values, axis=-1, keepdims=True)
    inv_std = lax.rsqrt(jnp.mean(center * center, axis=-1, keepdims=True) + eps_norm)
    return (center * inv_std, inv_std)


def norm_back(gradient, normed, inv_std):
    return inv_std * (
        gradient
        - jnp.mean(gradient, axis=-1, keepdims=True)
        - normed * jnp.mean(gradient * normed, axis=-1, keepdims=True)
    )


def head_norm(raw_vals):
    inv_std = lax.rsqrt(jnp.mean(raw_vals * raw_vals, axis=-1, keepdims=True) + eps_norm)
    return (raw_vals * inv_std, inv_std)


def head_back(gradient, unit_vals, inv_std):
    return inv_std * (gradient - unit_vals * jnp.mean(gradient * unit_vals, axis=-1, keepdims=True))


def gelu_both(pre_act):
    inner_arg = gelu_coef * (pre_act + 0.044715 * pre_act * pre_act * pre_act)
    tanh_val = jnp.tanh(inner_arg)
    act_value = 0.5 * pre_act * (1.0 + tanh_val)
    act_slope = 0.5 * (1.0 + tanh_val) + 0.5 * pre_act * (1.0 - tanh_val * tanh_val) * gelu_coef * (
        1.0 + 3.0 * 0.044715 * pre_act * pre_act
    )
    return (act_value, act_slope)


def rows_product(left_rows, right_rows):
    return lax.dot_general(
        left_rows, right_rows, (((0,), (0,)), ((), ())), preferred_element_type=jnp.float32
    )


def back_product(grad_rows, weight_mat):
    return lax.dot_general(
        grad_rows, weight_mat, (((1,), (1,)), ((), ())), preferred_element_type=jnp.float32
    )


def settle(first_grad, second_grad, third_grad):
    owned = (
        lax.psum_scatter(
            first_grad.astype(jnp.bfloat16), "dp", scatter_dimension=1, tiled=True
        ).astype(jnp.float32),
        lax.psum_scatter(
            second_grad.astype(jnp.bfloat16), "dp", scatter_dimension=1, tiled=True
        ).astype(jnp.float32),
        lax.psum_scatter(
            third_grad.astype(jnp.bfloat16), "dp", scatter_dimension=1, tiled=True
        ).astype(jnp.float32),
    )
    return (
        lax.psum(owned[0].astype(jnp.bfloat16), "seq").astype(jnp.float32),
        lax.psum(owned[1].astype(jnp.bfloat16), "seq").astype(jnp.float32),
        lax.psum(owned[2].astype(jnp.bfloat16), "seq").astype(jnp.float32),
    )


def body(
    image_in,
    text_in,
    image_cot,
    text_cot,
    cond_table,
    seq_table,
    text_count,
    mod_weight,
    mod_bias,
    qkv_weight,
    qkv_bias,
    qk_gain,
    out_weight,
    out_bias,
    up_weight,
    up_bias,
    down_weight,
    down_bias,
):
    seq_parts = lax.axis_size("seq")
    data_parts = lax.axis_size("dp")
    section_index = lax.axis_index("section")
    data_index = lax.axis_index("dp")
    seq_index = lax.axis_index("seq")
    first_section = section_index == 0
    batches = image_in.shape[0]
    image_rows = image_in.shape[2]
    text_rows = text_in.shape[2]
    model_width = image_in.shape[3]
    head_size = HD
    local_heads = HEADS // seq_parts
    image_keys = seq_parts * image_rows
    text_keys = seq_parts * text_rows

    def choose_by(flag, first_tree, second_tree):
        return jax.tree.map(
            lambda left_item, right_item: jnp.where(flag, left_item, right_item),
            first_tree,
            second_tree,
        )

    (
        mod_shift,
        qkv_full,
        qkv_shift,
        gain_full,
        out_full,
        out_shift,
        up_full,
        up_shift,
        down_full,
        down_shift,
    ) = (
        lax.all_gather(mod_bias, "dp", axis=2, tiled=True),
        lax.all_gather(qkv_weight, "dp", axis=2, tiled=True),
        lax.all_gather(qkv_bias, "dp", axis=2, tiled=True),
        lax.all_gather(qk_gain, "dp", axis=2, tiled=True),
        lax.all_gather(out_weight, "dp", axis=2, tiled=True),
        lax.all_gather(out_bias, "dp", axis=2, tiled=True),
        lax.all_gather(up_weight, "dp", axis=2, tiled=True),
        lax.all_gather(up_bias, "dp", axis=2, tiled=True),
        lax.all_gather(down_weight, "dp", axis=2, tiled=True),
        lax.all_gather(down_bias, "dp", axis=2, tiled=True),
    )
    all_cond = jax.nn.silu(
        jnp.take(cond_table, seq_table.reshape(-1), axis=0).astype(jnp.float32)
    ).astype(jnp.bfloat16)
    row_share = mod_weight.shape[2]
    cond_cols = lax.dynamic_slice_in_dim(all_cond, data_index * row_share, row_share, 1)
    partial_mod = jnp.einsum(
        "rd,sdk->rsk", cond_cols, mod_weight[0], preferred_element_type=jnp.float32
    )
    modulation = lax.psum_scatter(
        partial_mod.astype(jnp.bfloat16), "dp", scatter_dimension=0, tiled=True
    ).astype(jnp.float32)
    modulation = (modulation + mod_shift[0].astype(jnp.float32)[None]).reshape(
        batches, 2, 6, model_width
    )
    qkv_mats = qkv_full[0]
    qkv_add = qkv_shift[0].astype(jnp.float32)
    gain_rows = gain_full[0].astype(jnp.float32)
    out_mats = out_full[0]
    out_add = out_shift[0].astype(jnp.float32)
    up_mats = up_full[0]
    up_add = up_shift[0].astype(jnp.float32)
    down_mats = down_full[0]
    down_add = down_shift[0].astype(jnp.float32)
    own_counts = text_count[:, 0, :]
    text_pos = jnp.arange(text_rows)
    my_counts = lax.dynamic_index_in_dim(own_counts, seq_index, 1, keepdims=False)
    live_text = (text_pos[None, :] < my_counts[:, None]).astype(jnp.float32)
    live_keys = (
        (text_pos[None, None, :] < own_counts[:, :, None])
        .astype(jnp.float32)
        .reshape(batches, text_keys)
    )
    key_mask = jnp.concatenate([jnp.ones((batches, image_keys), jnp.float32), live_keys], axis=1)

    def spread_gain(offset):
        return jnp.concatenate(
            [
                jnp.broadcast_to(
                    gain_rows[0, offset : offset + head_size], (image_keys, head_size)
                ),
                jnp.broadcast_to(gain_rows[1, offset : offset + head_size], (text_keys, head_size)),
            ],
            axis=0,
        )[:, None, :]

    query_gain = spread_gain(0)
    key_gain = spread_gain(head_size)

    def head_inputs(joined):
        query_unit, query_inv = head_norm(joined[:, :, 0].astype(jnp.float32))
        key_unit, key_inv = head_norm(joined[:, :, 1].astype(jnp.float32))
        query_low = (query_unit * query_gain).astype(jnp.bfloat16)
        key_low = (key_unit * key_gain).astype(jnp.bfloat16)
        return (query_unit, query_inv, key_unit, key_inv, query_low, key_low)

    received = jnp.zeros((image_rows + text_rows, model_width), jnp.bfloat16)
    forward_saved = []
    forward_sent = []
    for tick_num in range(batches + 1):
        own_slot = min(tick_num, batches - 1)
        fresh = jnp.concatenate([image_in[own_slot, 0], text_in[own_slot, 0]], axis=0)
        chosen = jnp.where(first_section, fresh, received).astype(jnp.float32)
        slot_num = jnp.clip(tick_num - section_index, 0, batches - 1)
        inputs = (chosen[:image_rows], chosen[image_rows:])
        forward_mod_rows = modulation[slot_num]
        forward_live_row = live_text[slot_num]
        first_parts = []
        packed = []
        for forward_stream in range(2):
            forward_normed, forward_inv_std = layer_norm(inputs[forward_stream])
            forward_hidden = (
                forward_normed * (1.0 + forward_mod_rows[forward_stream, 1])
                + forward_mod_rows[forward_stream, 0]
            ).astype(jnp.bfloat16)
            projected = (
                jnp.dot(
                    forward_hidden, qkv_mats[forward_stream], preferred_element_type=jnp.float32
                )
                + qkv_add[forward_stream]
            )
            packed.append(projected.astype(jnp.bfloat16))
            first_parts.append((forward_normed, forward_inv_std, forward_hidden))
        forward_image_heads = lax.all_to_all(
            packed[0], "seq", split_axis=1, concat_axis=0, tiled=True
        )
        forward_text_heads = lax.all_to_all(
            packed[1], "seq", split_axis=1, concat_axis=0, tiled=True
        )
        forward_joined = jnp.concatenate([forward_image_heads, forward_text_heads], axis=0).reshape(
            -1, local_heads, 3, head_size
        )
        (
            forward_query_unit,
            forward_query_inv,
            forward_key_unit,
            forward_key_inv,
            forward_query_low,
            forward_key_low,
        ) = head_inputs(forward_joined)
        forward_scores = (
            jnp.einsum(
                "qhd,khd->hqk",
                forward_query_low,
                forward_key_low,
                preferred_element_type=jnp.float32,
            )
            * 0.125
        )
        exp_scores = jnp.exp(forward_scores) * key_mask[slot_num][None, None, :]
        denom_sum = jnp.sum(exp_scores, axis=-1, keepdims=True)
        probs_low = (exp_scores / denom_sum).astype(jnp.bfloat16)
        attended = jnp.einsum(
            "hqk,khd->qhd", probs_low, forward_joined[:, :, 2], preferred_element_type=jnp.float32
        ).astype(jnp.bfloat16)
        attended = attended.reshape(-1, local_heads * head_size)
        image_tok = lax.all_to_all(
            attended[:image_keys], "seq", split_axis=0, concat_axis=1, tiled=True
        )
        text_tok = lax.all_to_all(
            attended[image_keys:], "seq", split_axis=0, concat_axis=1, tiled=True
        )
        outputs = []
        forward_stream_saved = []
        for forward_stream in range(2):
            forward_normed, forward_inv_std, forward_hidden = first_parts[forward_stream]
            forward_attn_tok = (image_tok, text_tok)[forward_stream]
            forward_branch = (
                jnp.dot(
                    forward_attn_tok, out_mats[forward_stream], preferred_element_type=jnp.float32
                )
                + out_add[forward_stream]
            )
            middle = inputs[forward_stream] + forward_mod_rows[forward_stream, 2] * forward_branch
            forward_normed_mid, forward_inv_mid = layer_norm(middle)
            forward_hidden_mid = (
                forward_normed_mid * (1.0 + forward_mod_rows[forward_stream, 4])
                + forward_mod_rows[forward_stream, 3]
            ).astype(jnp.bfloat16)
            pre_act = (
                jnp.dot(
                    forward_hidden_mid, up_mats[forward_stream], preferred_element_type=jnp.float32
                )
                + up_add[forward_stream]
            )
            act_value, forward_act_slope = gelu_both(pre_act)
            forward_active = act_value.astype(jnp.bfloat16)
            forward_mlp_out = (
                jnp.dot(
                    forward_active, down_mats[forward_stream], preferred_element_type=jnp.float32
                )
                + down_add[forward_stream]
            )
            result = middle + forward_mod_rows[forward_stream, 5] * forward_mlp_out
            if forward_stream == 1:
                result = result * forward_live_row[:, None]
            outputs.append(result)
            forward_stream_saved.append(
                (
                    forward_normed,
                    forward_inv_std,
                    forward_hidden,
                    forward_attn_tok,
                    forward_branch,
                    forward_normed_mid,
                    forward_inv_mid,
                    forward_hidden_mid,
                    forward_act_slope,
                    forward_active,
                    forward_mlp_out,
                )
            )
        result_rows = jnp.concatenate(outputs, axis=0)
        saved_acts = (forward_stream_saved, forward_joined, jnp.log(denom_sum))
        sent_rows = result_rows.astype(jnp.bfloat16)
        forward_saved.append(saved_acts)
        forward_sent.append(sent_rows)
        if tick_num < batches:
            received = passed_along(sent_rows, "section", 1)
    cot_rows = jnp.concatenate([image_cot[:, 0], text_cot[:, 0]], axis=1)
    back_recv = jnp.zeros((image_rows + text_rows, model_width), jnp.bfloat16)
    back_saved = []
    back_inputs = []
    for tick_num in range(batches + 1):
        slot_num = jnp.clip(tick_num - 1 + section_index, 0, batches - 1)
        incoming = jnp.where(first_section, back_recv, cot_rows[min(tick_num, batches - 1)]).astype(
            jnp.float32
        )
        saved_acts = choose_by(
            first_section,
            forward_saved[max(tick_num - 1, 0)],
            forward_saved[min(tick_num + 1, batches)],
        )
        mod_rows = modulation[slot_num]
        live_row = live_text[slot_num]
        stream_saved, backward_joined, log_denom = saved_acts
        grad_parts = (incoming[:image_rows], incoming[image_rows:])
        attn_grads = []
        kept_grads = []
        for backward_stream in range(2):
            (
                normed,
                inv_std,
                hidden,
                attn_tok,
                branch,
                normed_mid,
                inv_mid,
                hidden_mid,
                act_slope,
                active,
                mlp_out,
            ) = stream_saved[backward_stream]
            grad_out = grad_parts[backward_stream]
            if backward_stream == 1:
                grad_out = grad_out * live_row[:, None]
            gate_two = jnp.sum(grad_out * mlp_out, axis=0)
            mlp_grad = (mod_rows[backward_stream, 5] * grad_out).astype(jnp.bfloat16)
            pre_grad = (back_product(mlp_grad, down_mats[backward_stream]) * act_slope).astype(
                jnp.bfloat16
            )
            hidden_grad = back_product(pre_grad, up_mats[backward_stream])
            scale_two = jnp.sum(hidden_grad * normed_mid, axis=0)
            shift_two = jnp.sum(hidden_grad, axis=0)
            middle_grad = grad_out + norm_back(
                hidden_grad * (1.0 + mod_rows[backward_stream, 4]), normed_mid, inv_mid
            )
            gate_one = jnp.sum(middle_grad * branch, axis=0)
            branch_grad = (mod_rows[backward_stream, 2] * middle_grad).astype(jnp.bfloat16)
            attn_grads.append(
                back_product(branch_grad, out_mats[backward_stream]).astype(jnp.bfloat16)
            )
            kept_grads.append(
                (
                    middle_grad,
                    gate_one,
                    shift_two,
                    scale_two,
                    gate_two,
                    branch_grad,
                    pre_grad,
                    mlp_grad,
                )
            )
        image_heads = lax.all_to_all(attn_grads[0], "seq", split_axis=1, concat_axis=0, tiled=True)
        text_heads = lax.all_to_all(attn_grads[1], "seq", split_axis=1, concat_axis=0, tiled=True)
        out_grad = jnp.concatenate([image_heads, text_heads], axis=0).reshape(
            -1, local_heads, head_size
        )
        (
            backward_query_unit,
            backward_query_inv,
            backward_key_unit,
            backward_key_inv,
            backward_query_low,
            backward_key_low,
        ) = head_inputs(backward_joined)
        value_rows = backward_joined[:, :, 2]
        scores = (
            jnp.einsum(
                "qhd,khd->hqk",
                backward_query_low,
                backward_key_low,
                preferred_element_type=jnp.float32,
            )
            * 0.125
        )
        probs = jnp.exp(scores - log_denom) * key_mask[slot_num][None, None, :]
        prob_grad = jnp.einsum(
            "qhd,khd->hqk", out_grad, value_rows, preferred_element_type=jnp.float32
        )
        row_dot = jnp.sum(probs * prob_grad, axis=-1, keepdims=True)
        score_grad = (probs * (prob_grad - row_dot)).astype(jnp.bfloat16)
        value_grad = jnp.einsum(
            "hqk,qhd->khd", probs.astype(jnp.bfloat16), out_grad, preferred_element_type=jnp.float32
        )
        query_grad = (
            jnp.einsum(
                "hqk,khd->qhd", score_grad, backward_key_low, preferred_element_type=jnp.float32
            )
            * 0.125
        )
        key_grad = (
            jnp.einsum(
                "hqk,qhd->khd", score_grad, backward_query_low, preferred_element_type=jnp.float32
            )
            * 0.125
        )
        query_sums = jnp.sum(query_grad * backward_query_unit, axis=1)
        key_sums = jnp.sum(key_grad * backward_key_unit, axis=1)
        gain_grad = jnp.stack(
            [
                jnp.concatenate(
                    [
                        jnp.sum(query_sums[:image_keys], axis=0),
                        jnp.sum(key_sums[:image_keys], axis=0),
                    ]
                ),
                jnp.concatenate(
                    [
                        jnp.sum(query_sums[image_keys:], axis=0),
                        jnp.sum(key_sums[image_keys:], axis=0),
                    ]
                ),
            ]
        )
        packed_grad = (
            jnp.stack(
                [
                    head_back(query_grad * query_gain, backward_query_unit, backward_query_inv),
                    head_back(key_grad * key_gain, backward_key_unit, backward_key_inv),
                    value_grad,
                ],
                axis=2,
            )
            .astype(jnp.bfloat16)
            .reshape(-1, local_heads * 3 * head_size)
        )
        image_qkv = lax.all_to_all(
            packed_grad[:image_keys], "seq", split_axis=0, concat_axis=1, tiled=True
        )
        text_qkv = lax.all_to_all(
            packed_grad[image_keys:], "seq", split_axis=0, concat_axis=1, tiled=True
        )
        input_grads = []
        mod_grads = []
        pieces = []
        for backward_stream in range(2):
            normed = stream_saved[backward_stream][0]
            inv_std = stream_saved[backward_stream][1]
            (
                middle_grad,
                gate_one,
                shift_two,
                scale_two,
                gate_two,
                branch_grad,
                pre_grad,
                mlp_grad,
            ) = kept_grads[backward_stream]
            qkv_grad = (image_qkv, text_qkv)[backward_stream]
            hidden_grad = back_product(qkv_grad, qkv_mats[backward_stream])
            scale_one = jnp.sum(hidden_grad * normed, axis=0)
            shift_one = jnp.sum(hidden_grad, axis=0)
            input_grads.append(
                middle_grad
                + norm_back(hidden_grad * (1.0 + mod_rows[backward_stream, 1]), normed, inv_std)
            )
            mod_grads.append(
                jnp.stack([shift_one, scale_one, gate_one, shift_two, scale_two, gate_two])
            )
            pieces.append((qkv_grad, branch_grad, pre_grad, mlp_grad))
        grad_rows, mod_grad, gain_grad, pieces = (
            jnp.concatenate(input_grads, axis=0),
            jnp.stack(mod_grads),
            gain_grad,
            pieces,
        )
        sent_back = grad_rows.astype(jnp.bfloat16)
        back_inputs.append((grad_rows, sent_back))
        back_saved.append((mod_grad, gain_grad, pieces))
        if tick_num < batches:
            back_recv = passed_along(sent_back, "section", -1)
    act_list = []
    grad_list = []
    for slot_pos in range(batches):
        act_list.append(
            jnp.where(first_section, forward_sent[slot_pos], forward_sent[slot_pos + 1])
        )
        grad_list.append(
            jnp.where(
                first_section,
                back_inputs[slot_pos + 1][0],
                back_inputs[slot_pos][1].astype(jnp.float32),
            )
        )
    act_all = jnp.stack(act_list)
    grad_all = jnp.stack(grad_list)
    image_out = act_all[:, :image_rows][None, :, None]
    text_out = act_all[:, image_rows:][None, :, None]
    image_grad = grad_all[:, :image_rows][None, :, None]
    text_grad = grad_all[:, image_rows:][None, :, None]
    inputs_by = [[[], [], [], []], [[], [], [], []]]
    grads_by = [[[], [], [], []], [[], [], [], []]]
    mod_list = []
    gain_total = jnp.zeros((2, 2 * head_size), jnp.float32)
    for slot_pos in range(batches):
        mod_grad, gain_grad, pieces = choose_by(
            first_section, back_saved[slot_pos + 1], back_saved[slot_pos]
        )
        mod_list.append(mod_grad)
        gain_total = gain_total + gain_grad
        for stream in range(2):
            early_acts = forward_saved[slot_pos][0][stream]
            later_acts = forward_saved[slot_pos + 1][0][stream]
            for field_num, stash_num in enumerate((2, 3, 7, 9)):
                inputs_by[stream][field_num].append(
                    jnp.where(first_section, early_acts[stash_num], later_acts[stash_num])
                )
                grads_by[stream][field_num].append(pieces[stream][field_num])
    settled = []
    for stream in range(2):
        products = []
        biases = []
        for field_num in range(4):
            left_rows = jnp.concatenate(inputs_by[stream][field_num], axis=0)
            right_rows = jnp.concatenate(grads_by[stream][field_num], axis=0)
            products.append(rows_product(left_rows, right_rows)[None])
            biases.append(jnp.sum(right_rows.astype(jnp.float32), axis=0)[None])
        qkv_part, qkvb_part, gain_part = settle(products[0], biases[0], gain_total[stream][None])
        outw_part, outb_part, upb_part = settle(products[1], biases[1], biases[2])
        upw_part, downw_part, downb_part = settle(products[2], products[3], biases[3])
        settled.append(
            (
                qkv_part,
                qkvb_part,
                gain_part,
                outw_part,
                outb_part,
                upw_part,
                upb_part,
                downw_part,
                downb_part,
            )
        )

    def join_streams(field_num):
        return jnp.stack([settled[0][field_num], settled[1][field_num]], axis=1)

    mod_stack = jnp.stack(mod_list).reshape(batches, 2, 6 * model_width)
    every_mod = lax.all_gather(
        mod_stack.astype(jnp.bfloat16), ("dp", "seq"), axis=0, tiled=True
    ).astype(mod_stack.dtype)
    every_mod = every_mod.reshape(data_parts, seq_parts, batches, 2, 6 * model_width).sum(axis=1)
    every_mod = every_mod.reshape(data_parts * batches, 2, 6 * model_width)
    modw_grad = jnp.einsum(
        "rd,rsk->sdk", cond_cols.astype(jnp.float32), every_mod, precision=lax.Precision.HIGHEST
    )[None]
    bias_share = mod_bias.shape[2]
    modb_grad = lax.dynamic_slice_in_dim(
        jnp.sum(every_mod, axis=0), data_index * bias_share, bias_share, 1
    )[None]
    return (
        image_out,
        text_out,
        image_grad,
        text_grad,
        modw_grad,
        modb_grad,
        join_streams(0),
        join_streams(1),
        join_streams(2),
        join_streams(3),
        join_streams(4),
        join_streams(5),
        join_streams(6),
        join_streams(7),
        join_streams(8),
    )


def solution(mesh):
    return jax.shard_map(
        body,
        mesh=mesh,
        in_specs=(
            P(None, "dp", "seq", None),
            P(None, "dp", "seq", None),
            P(None, "dp", "seq", None),
            P(None, "dp", "seq", None),
            P(),
            P(),
            P(None, "dp", None),
            P("section", None, "dp", None),
            P("section", None, "dp"),
            P("section", None, "dp", None),
            P("section", None, "dp"),
            P("section", None, "dp"),
            P("section", None, "dp", None),
            P("section", None, "dp"),
            P("section", None, "dp", None),
            P("section", None, "dp"),
            P("section", None, "dp", None),
            P("section", None, "dp"),
        ),
        out_specs=(
            P("section", None, "dp", "seq", None),
            P("section", None, "dp", "seq", None),
            P("section", None, "dp", "seq", None),
            P("section", None, "dp", "seq", None),
            P("section", None, "dp", None),
            P("section", None, "dp"),
            P("section", None, "dp", None),
            P("section", None, "dp"),
            P("section", None, "dp"),
            P("section", None, "dp", None),
            P("section", None, "dp"),
            P("section", None, "dp", None),
            P("section", None, "dp"),
            P("section", None, "dp", None),
            P("section", None, "dp"),
        ),
        check_vma=False,
    )
```

profile of v0, /device:TPU:0, one launch (start us, length us, event | category | flops | bytes accessed | tf_op | source)
XLA Modules:
  0.0 5710.4 jit_solution(9972583484498970756)
XLA Ops:
  17.6 32.5 all_gather.36
  50.6 34.0 all_gather.42
  86.1 106.0 %all_gather.35 = bf16[1,2,4608]{1,0,2:T(2,128)(2,1)S(1)} all-gather(bf16[1,2,576]{1,0,2:T(2,128)(2,1)S(1)} %copy.281), channel_id=1, replica_groups=mesh['section'=2,'dp'=8,'seq'=2] {'dp'}, dimensions={2}, use_global_device_ids=true | all-gather | bytes 20736 | tf_op jit(solution)/shard_map/all_gather | solution.py:140
  196.1 40.2 all_gather.40
  236.3 49.6 all_gather.33
  290.4 25.3 slice_reduce_fusion.4
  315.8 75.5 %slice_reduce_fusion = (f32[4608]{0:T(1024)S(1)}, f32[4608]{0:T(1024)S(1)}) fusion(f32[1,2,4608]{1,0,2:T(1,128)S(1)} %convert_element_type.645), kind=kLoop, calls=%fused_computation.100 | loop fusion | bytes 73728 | tf_op jit(solution)/shard_map/slice | solution.py:227
  394.9 263.1 %all-gather.6.cloned.1.call-done = bf16[1,2,1536,4608]{3,2,1,0:T(8,128)(2,1)} async-done(((bf16[1,2,192,4608]{3,2,1,0:T(8,128)(2,1)}), bf16[1,2,1536,4608]{3,2,1,0:T(8,128)(2,1)}) %all-gather.6.cloned.1.call-update) | async-done | bytes 28311568 | tf_op jit(solution)/shard_map/all_gather | solution.py:139
  682.3 35.7 all_gather.38
  718.8 24.8 slice_reduce_fusion.5
  766.8 37.8 all-gather.8.cloned.1.call-done
  813.8 706.6 %all-gather.10.cloned.1.call-done = bf16[1,2,1536,6144]{3,2,1,0:T(8,128)(2,1)} async-done(((bf16[1,2,192,6144]{3,2,1,0:T(8,128)(2,1)}), bf16[1,2,1536,6144]{3,2,1,0:T(8,128)(2,1)}) %all-gather.10.cloned.1.call-update) | async-done | bytes 37748752 | tf_op jit(solution)/shard_map/all_gather | solution.py:144
  1528.7 10.8 fusion.34
  1539.5 698.6 %all-gather.12.cloned.1.call-done = bf16[1,2,6144,1536]{3,2,1,0:T(8,128)(2,1)} async-done(((bf16[1,2,768,1536]{3,2,1,0:T(8,128)(2,1)}), bf16[1,2,6144,1536]{3,2,1,0:T(8,128)(2,1)}) %all-gather.12.cloned.1.call-update) | async-done | bytes 37748752 | tf_op jit(solution)/shard_map/all_gather | solution.py:146
  2238.2 11.0 add_convert_fusion.7
  2336.5 10.4 fusion.48
  2347.0 11.1 multiply_reduce_fusion.38
  2391.6 11.8 multiply_reduce_fusion.8
  2569.1 10.3 broadcast_select_fusion.4
  2582.0 11.1 fusion.47
  2593.2 13.6 multiply_reduce_fusion.42
  2620.5 11.4 fusion.38
  2632.0 10.7 multiply_reduce_fusion.12
  2710.0 12.2 fusion.403
  2722.3 13.3 fusion.6
  2735.7 10.6 multiply_reduce_fusion.7
  2752.9 13.2 fusion.405
  2766.2 10.3 multiply_reduce_fusion.34
  2855.1 10.9 fusion.2
  2912.3 10.3 multiply_reduce_fusion.37
  2959.8 221.1 %reduce-scatter.42.cloned.1.call-done = bf16[1,192,4608]{2,1,0:T(8,128)(2,1)} async-done(((bf16[1,1536,4608]{2,1,0:T(8,128)(2,1)}), bf16[1,192,4608]{2,1,0:T(8,128)(2,1)}) %reduce-scatter.42.cloned.1.call-update) | async-done | bytes 1769488 | tf_op jit(solution)/shard_map/reduce_scatter | solution.py:67
  3180.9 232.2 %reduce-scatter.40.cloned.1.call-done = bf16[1,192,4608]{2,1,0:T(8,128)(2,1)} async-done(((bf16[1,1536,4608]{2,1,0:T(8,128)(2,1)}), bf16[1,192,4608]{2,1,0:T(8,128)(2,1)}) %reduce-scatter.40.cloned.1.call-update) | async-done | bytes 1769488 | tf_op jit(solution)/shard_map/reduce_scatter | solution.py:67
  3413.1 312.7 %reduce-scatter.52.cloned.1.call-done = bf16[1,768,1536]{2,1,0:T(8,128)(2,1)} async-done(((bf16[1,6144,1536]{2,1,0:T(8,128)(2,1)}), bf16[1,768,1536]{2,1,0:T(8,128)(2,1)}) %reduce-scatter.52.cloned.1.call-update) | async-done | bytes 2359312 | tf_op jit(solution)/shard_map/reduce_scatter | solution.py:70
  3725.7 312.8 %reduce-scatter.54.cloned.1.call-done = bf16[1,768,1536]{2,1,0:T(8,128)(2,1)} async-done(((bf16[1,6144,1536]{2,1,0:T(8,128)(2,1)}), bf16[1,768,1536]{2,1,0:T(8,128)(2,1)}) %reduce-scatter.54.cloned.1.call-update) | async-done | bytes 2359312 | tf_op jit(solution)/shard_map/reduce_scatter | solution.py:70
  4038.6 312.5 %reduce-scatter.48.cloned.1.call-done = bf16[1,192,6144]{2,1,0:T(8,128)(2,1)} async-done(((bf16[1,1536,6144]{2,1,0:T(8,128)(2,1)}), bf16[1,192,6144]{2,1,0:T(8,128)(2,1)}) %reduce-scatter.48.cloned.1.call-update) | async-done | bytes 2359312 | tf_op jit(solution)/shard_map/reduce_scatter | solution.py:67
  4351.1 312.6 %reduce-scatter.50.cloned.1.call-done = bf16[1,192,6144]{2,1,0:T(8,128)(2,1)} async-done(((bf16[1,1536,6144]{2,1,0:T(8,128)(2,1)}), bf16[1,192,6144]{2,1,0:T(8,128)(2,1)}) %reduce-scatter.50.cloned.1.call-update) | async-done | bytes 2359312 | tf_op jit(solution)/shard_map/reduce_scatter | solution.py:67
  4666.6 61.6 %reduce-scatter.72.cloned.1.call-done = bf16[192,1]{1,0:T(8,128)(2,1)} async-done(((bf16[1536,1]{1,0:T(8,128)(2,1)}), bf16[192,1]{1,0:T(8,128)(2,1)}) %reduce-scatter.72.cloned.1.call-update) | async-done | bytes 400
  4729.0 63.5 %reduce-scatter.64.cloned.1.call-done = bf16[192,1]{1,0:T(8,128)(2,1)} async-done(((bf16[1536,1]{1,0:T(8,128)(2,1)}), bf16[192,1]{1,0:T(8,128)(2,1)}) %reduce-scatter.64.cloned.1.call-update) | async-done | bytes 400
  4793.4 63.5 %reduce-scatter.74.cloned.1.call-done = bf16[192,1]{1,0:T(8,128)(2,1)} async-done(((bf16[1536,1]{1,0:T(8,128)(2,1)}), bf16[192,1]{1,0:T(8,128)(2,1)}) %reduce-scatter.74.cloned.1.call-update) | async-done | bytes 400
  4857.8 63.4 %reduce-scatter.66.cloned.1.call-done = bf16[192,1]{1,0:T(8,128)(2,1)} async-done(((bf16[1536,1]{1,0:T(8,128)(2,1)}), bf16[192,1]{1,0:T(8,128)(2,1)}) %reduce-scatter.66.cloned.1.call-update) | async-done | bytes 400
  4922.1 67.5 %reduce-scatter.68.cloned.1.call-done = bf16[768,1]{1,0:T(8,128)(2,1)} async-done(((bf16[6144,1]{1,0:T(8,128)(2,1)}), bf16[768,1]{1,0:T(8,128)(2,1)}) %reduce-scatter.68.cloned.1.call-update) | async-done | bytes 1552
  4990.6 67.3 %reduce-scatter.70.cloned.1.call-done = bf16[768,1]{1,0:T(8,128)(2,1)} async-done(((bf16[6144,1]{1,0:T(8,128)(2,1)}), bf16[768,1]{1,0:T(8,128)(2,1)}) %reduce-scatter.70.cloned.1.call-update) | async-done | bytes 1552
  5059.0 55.7 reduce-scatter.60.cloned.1.call-done
  5115.4 56.2 reduce-scatter.62.cloned.1.call-done
  5172.4 66.2 %reduce-scatter.58.cloned.1.call-done = bf16[576,1]{1,0:T(8,128)(2,1)} async-done(((bf16[4608,1]{1,0:T(8,128)(2,1)}), bf16[576,1]{1,0:T(8,128)(2,1)}) %reduce-scatter.58.cloned.1.call-update) | async-done | bytes 1168
  5241.5 64.2 %reduce-scatter.56.cloned.1.call-done = bf16[576,1]{1,0:T(8,128)(2,1)} async-done(((bf16[4608,1]{1,0:T(8,128)(2,1)}), bf16[576,1]{1,0:T(8,128)(2,1)}) %reduce-scatter.56.cloned.1.call-update) | async-done | bytes 1168
  5318.0 45.3 all-gather.14.cloned.1.call-done
  5378.0 309.0 %all-reduce.9.cloned.1.call-done = (bf16[1,1,192,4608]{3,2,1,0:T(8,128)(2,1)}, bf16[1,1,192,4608]{3,2,1,0:T(8,128)(2,1)}, bf16[1,1,192,1536]{3,2,1,0:T(8,128)(2,...) async-done(((bf16[1,1,192,4608]{3,2,1,0:T(8,128)(2,1)}, ...) | async-done | bytes 14155792 | tf_op jit(solution)/shard_map/psum | solution.py:78
  (1494 shorter events, 678.8 us)
Async XLA Ops:
  7.2 384.9 %all-reduce.7.cloned.1.call-start = ((), (), s32[]{:S(2)}) async-start(), calls=%async_computation.65 | async-start | bytes 1179648
  14.5 643.5 %all-gather.6.cloned.1.call-start = ((), (), s32[]{:S(2)}) async-start(), calls=%async_computation.42 | async-start | bytes 31850496 | tf_op jit(solution)/shard_map/all_gather | solution.py:139
  15.2 789.3 %all-gather.8.cloned.1.call-start = ((), (), s32[]{:S(2)}) async-start(), calls=%async_computation.43 | async-start | bytes 10616832 | tf_op jit(solution)/shard_map/all_gather | solution.py:142
  16.0 1504.5 %all-gather.10.cloned.1.call-start = ((), (), s32[]{:S(2)}) async-start(), calls=%async_computation.44 | async-start | bytes 42467328 | tf_op jit(solution)/shard_map/all_gather | solution.py:144
  16.6 2221.6 %all-gather.12.cloned.1.call-start = ((), (), s32[]{:S(2)}) async-start(), calls=%async_computation.45 | async-start | bytes 42467328 | tf_op jit(solution)/shard_map/all_gather | solution.py:146
  665.2 12.8 all-to-all-start.1
  678.0 66.7 %all-to-all-start = ((bf16[64,2,2304]{2,0,1:T(8,128)(2,1)}), bf16[64,2,2304]{2,0,1:T(8,128)(2,1)S(1)}, u32[]{:S(2)}, u32[]{:S(2)}) async-start(bf16[64,2,2304]{2,0,1:T(8,128)(2,1)} %bitcast.719), calls=%async_computation | async-start | bytes 1179648 | tf_op jit(solution)/shard_map/all_to_all | solution.py:231
  763.3 45.6 all-to-all-start.2
  2270.3 13.0 all-to-all-start.5
  2283.3 13.0 all-to-all-start.4
  2309.5 48.6 all-to-all-start.6
  2415.3 12.1 all-to-all-start.9
  2427.3 13.2 all-to-all-start.8
  2455.9 8.4 all-to-all-start.11
  2464.3 15.8 all-to-all-start.10
  2480.1 15.1 all-to-all-start.13
  2495.3 9.0 all-to-all-start.12
  2520.5 22.3 all-to-all-start.15
  2542.8 14.2 all-to-all-start.14
  2567.7 11.8 collective-permute-start.2
  2615.1 31.5 all-to-all-start.17
  2646.6 8.9 all-to-all-start.16
  2668.9 13.0 all-to-all-start.19
  2681.9 12.9 all-to-all-start.18
  2685.4 274.4 %reduce-scatter.44.cloned.1.call-start = ((), (), s32[]{:S(2)}) async-start(), calls=%async_computation.49 | async-start | bytes 5308416 | tf_op jit(solution)/shard_map/reduce_scatter | solution.py:67
  2751.6 208.2 %reduce-scatter.46.cloned.1.call-start = ((), (), s32[]{:S(2)}) async-start(), calls=%async_computation.50 | async-start | bytes 5308416 | tf_op jit(solution)/shard_map/reduce_scatter | solution.py:67
  2787.5 8.0 all-to-all-start.21
  2795.5 8.5 all-to-all-start.20
  2812.4 8.9 all-to-all-start.23
  2816.0 364.9 %reduce-scatter.42.cloned.1.call-start = ((), (), s32[]{:S(2)}) async-start(), calls=%async_computation.48 | async-start | bytes 15925248 | tf_op jit(solution)/shard_map/reduce_scatter | solution.py:67
  2834.4 11.3 all-to-all-start.22
  2838.1 575.0 %reduce-scatter.40.cloned.1.call-start = ((), (), s32[]{:S(2)}) async-start(), calls=%async_computation.47 | async-start | bytes 15925248 | tf_op jit(solution)/shard_map/reduce_scatter | solution.py:67
  2853.8 871.9 %reduce-scatter.52.cloned.1.call-start = ((), (), s32[]{:S(2)}) async-start(), calls=%async_computation.53 | async-start | bytes 21233664 | tf_op jit(solution)/shard_map/reduce_scatter | solution.py:70
  2866.0 1172.6 %reduce-scatter.54.cloned.1.call-start = ((), (), s32[]{:S(2)}) async-start(), calls=%async_computation.54 | async-start | bytes 21233664 | tf_op jit(solution)/shard_map/reduce_scatter | solution.py:70
  2876.3 1474.8 %reduce-scatter.48.cloned.1.call-start = ((), (), s32[]{:S(2)}) async-start(), calls=%async_computation.51 | async-start | bytes 21233664 | tf_op jit(solution)/shard_map/reduce_scatter | solution.py:67
  2888.0 1775.7 %reduce-scatter.50.cloned.1.call-start = ((), (), s32[]{:S(2)}) async-start(), calls=%async_computation.52 | async-start | bytes 21233664 | tf_op jit(solution)/shard_map/reduce_scatter | solution.py:67
  2898.8 1829.3 %reduce-scatter.72.cloned.1.call-start = ((), (), s32[]{:S(2)}) async-start(), calls=%async_computation.63 | async-start | bytes 442368
  2906.6 1886.0 %reduce-scatter.64.cloned.1.call-start = ((), (), s32[]{:S(2)}) async-start(), calls=%async_computation.59 | async-start | bytes 442368
  2907.7 1949.2 %reduce-scatter.74.cloned.1.call-start = ((), (), s32[]{:S(2)}) async-start(), calls=%async_computation.64 | async-start | bytes 442368
  2908.8 2012.4 %reduce-scatter.66.cloned.1.call-start = ((), (), s32[]{:S(2)}) async-start(), calls=%async_computation.60 | async-start | bytes 442368
  2910.2 2079.4 %reduce-scatter.68.cloned.1.call-start = ((), (), s32[]{:S(2)}) async-start(), calls=%async_computation.61 | async-start | bytes 1769472
  2912.1 2145.8 %reduce-scatter.70.cloned.1.call-start = ((), (), s32[]{:S(2)}) async-start(), calls=%async_computation.62 | async-start | bytes 1769472
  2927.6 2187.1 %reduce-scatter.60.cloned.1.call-start = ((), (), s32[]{:S(2)}) async-start(), calls=%async_computation.57 | async-start | bytes 36864
  2929.0 2242.6 %reduce-scatter.62.cloned.1.call-start = ((), (), s32[]{:S(2)}) async-start(), calls=%async_computation.58 | async-start | bytes 36864
  2932.2 2306.4 %reduce-scatter.58.cloned.1.call-start = ((), (), s32[]{:S(2)}) async-start(), calls=%async_computation.56 | async-start | bytes 1327104
  2944.1 2361.6 %reduce-scatter.56.cloned.1.call-start = ((), (), s32[]{:S(2)}) async-start(), calls=%async_computation.55 | async-start | bytes 1327104
  2958.7 2404.6 %all-gather.14.cloned.1.call-start = ((), (), s32[]{:S(2)}) async-start(), calls=%async_computation.46 | async-start | bytes 1253376 | tf_op jit(solution)/shard_map/all_gather | solution.py:578
  2959.7 2727.2 %all-reduce.9.cloned.1.call-start = ((), (), s32[]{:S(2)}) async-start(), calls=%async_computation.66 | async-start | bytes 28311552 | tf_op jit(solution)/shard_map/psum | solution.py:78
  (474 other events, 23258.4 us)
Sparse Core Ops, SparseCore 0:
  14.6 79.0 all-reduce.6
  95.3 562.6 all-gather.5
  660.2 144.3 all-gather.7
  805.9 714.4 all-gather.9
  1521.8 716.2 all-gather.11
  2751.7 96.3 reduce-scatter.43
  2852.3 95.3 reduce-scatter.45
  2951.9 228.9 reduce-scatter.41
  3184.6 228.4 reduce-scatter.39
  3416.8 308.9 reduce-scatter.51
  3729.6 308.9 reduce-scatter.53
  4042.3 308.7 reduce-scatter.47
  4355.0 308.7 reduce-scatter.49
  4666.9 61.2 reduce-scatter.71
  4731.3 61.2 reduce-scatter.63
  4795.7 61.2 reduce-scatter.73
  4860.0 61.1 reduce-scatter.65
  4925.1 64.4 reduce-scatter.67
  4993.6 64.3 reduce-scatter.69
  5060.9 53.6 reduce-scatter.59
  5117.8 53.7 reduce-scatter.61
  5175.0 63.5 reduce-scatter.57
  5242.0 63.6 reduce-scatter.55
  5308.4 54.8 all-gather.13
  5366.2 320.6 all-reduce.8
where the time goes:
time: 5720 us; the launch traced here: 5710 us
  waiting for transfers between devices  4440 us (78%)
  matrix products  484 us (8%)
  blocking collectives  306 us (5%)
  local copies, waits for them, and re-layouts  280 us (5%)
  starting transfers between devices  94.8 us (2%)
  other arithmetic  87.5 us (2%)
    reduce_scatter x6, waiting for transfers between devices, settle(): lax.psum_scatter(first_grad.astype(jnp.bfloat16), 'dp', scatter_dimension...  1080 us
    all_gather x1, waiting for transfers between devices, body(): lax.all_gather(up_weight, 'dp', axis=2, tiled=True)  707 us
    all_gather x1, waiting for transfers between devices, body(): lax.all_gather(down_weight, 'dp', axis=2, tiled=True)  699 us
    unnamed x36, waiting for transfers between devices  632 us
    reduce_scatter x2, waiting for transfers between devices, settle(): lax.psum_scatter(second_grad.astype(jnp.bfloat16), 'dp', scatter_dimensio...  625 us
    psum x1, waiting for transfers between devices, settle(): lax.psum(owned[0].astype(jnp.bfloat16), 'seq').astype(jnp.float32)  309 us
    all_gather x1, waiting for transfers between devices, body(): lax.all_gather(qkv_weight, 'dp', axis=2, tiled=True)  263 us
    dot_general x24, matrix products, back_product(): lax.dot_general(grad_rows, weight_mat, (((1,), (1,)), ((), ())), preferre...  210 us
  transfers between devices with their start and end apart: 53, of which 35 were waited for; matrix products, arithmetic and copies ran while one was open for 10% of the time, Pallas kernels for 0%

commit v1 on v0

v1 whole, which is shorter than its diff:
```python
import functools

import jax
import jax.numpy as jnp
from jax import lax
from jax.experimental import pallas as pl
from jax.experimental.pallas import tpu as pltpu
from jax.sharding import PartitionSpec as P

HEADS = 24
HD = 64
TP = 8


eps_norm = 1e-06
gelu_coef = 0.7978845608028654
MESH = pl.DeviceIdType.MESH


def layer_norm(values):
    center = values - jnp.mean(values, axis=-1, keepdims=True)
    inv_std = lax.rsqrt(jnp.mean(center * center, axis=-1, keepdims=True) + eps_norm)
    return (center * inv_std, inv_std)


def norm_back(gradient, normed, inv_std):
    return inv_std * (
        gradient
        - jnp.mean(gradient, axis=-1, keepdims=True)
        - normed * jnp.mean(gradient * normed, axis=-1, keepdims=True)
    )


def head_norm(raw_vals):
    inv_std = lax.rsqrt(jnp.mean(raw_vals * raw_vals, axis=-1, keepdims=True) + eps_norm)
    return (raw_vals * inv_std, inv_std)


def head_back(gradient, unit_vals, inv_std):
    return inv_std * (gradient - unit_vals * jnp.mean(gradient * unit_vals, axis=-1, keepdims=True))


def gelu_both(pre_act):
    inner_arg = gelu_coef * (pre_act + 0.044715 * pre_act * pre_act * pre_act)
    tanh_val = jnp.tanh(inner_arg)
    act_value = 0.5 * pre_act * (1.0 + tanh_val)
    act_slope = 0.5 * (1.0 + tanh_val) + 0.5 * pre_act * (1.0 - tanh_val * tanh_val) * gelu_coef * (
        1.0 + 3.0 * 0.044715 * pre_act * pre_act
    )
    return (act_value, act_slope)


def mat(left, right):
    return lax.dot_general(
        left, right, (((1,), (0,)), ((), ())), preferred_element_type=jnp.float32
    )


def rows_product(left_rows, right_rows):
    return lax.dot_general(
        left_rows, right_rows, (((0,), (0,)), ((), ())), preferred_element_type=jnp.float32
    )


def back_product(grad_rows, weight_mat):
    return lax.dot_general(
        grad_rows, weight_mat, (((1,), (1,)), ((), ())), preferred_element_type=jnp.float32
    )


def ring_place(tp):
    row, col = (tp // 2, tp % 2)
    return row + col * (TP - 1 - 2 * row)


def ring_member(place):
    far = place // (TP // 2)
    row = place + far * (TP - 1 - 2 * place)
    return 2 * row + far


def ring_of(groups):
    dp_index = lax.axis_index("dp")
    sense = 1 - 2 * lax.axis_index("section")
    place = ring_place(dp_index // groups)
    group = dp_index % groups

    def member(steps):
        return ring_member((place + 2 * TP + sense * steps) % TP)

    sides = (member(1) * groups + group, member(-1) * groups + group)
    return (member, sides)


def greet(sides):
    barrier = pltpu.get_barrier_semaphore()
    for side in sides:
        pl.semaphore_signal(barrier, inc=1, device_id={"dp": side}, device_id_type=MESH)
    pl.semaphore_wait(barrier, 2)


def gather_kernel(groups, img_ref, txt_ref, img_out, txt_out, send_sem, recv_sem):
    member, sides = ring_of(groups)
    half = img_ref.shape[0] // 2
    pieces = ((img_ref, img_out, 0), (img_ref, img_out, half), (txt_ref, txt_out, 0))

    def copy_of(side, hop, piece):
        source_ref, target_ref, start = pieces[piece]
        origin = member(-hop if side == 0 else hop)
        rows = pl.ds(start, half)
        source = source_ref.at[rows] if hop == 0 else target_ref.at[origin, rows]
        return pltpu.make_async_remote_copy(
            src_ref=source,
            dst_ref=target_ref.at[origin, rows],
            send_sem=send_sem.at[side, hop, piece],
            recv_sem=recv_sem.at[side, hop, piece],
            device_id={"dp": sides[side]},
            device_id_type=MESH,
        )

    def moves(side, hop, piece):
        return hop < 3 or (piece < 2) == (side == 0)

    greet(sides)
    for hop in range(4):
        for piece in range(3):
            for side in range(2):
                if moves(side, hop, piece):
                    if hop > 0:
                        copy_of(side, hop - 1, piece).wait_recv()
                    copy_of(side, hop, piece).start()
        if hop == 0:
            me = member(0)
            img_out[me] = img_ref[...]
            txt_out[me] = txt_ref[...]
    for piece in range(3):
        for side in range(2):
            copy_of(side, 3 if moves(side, 3, piece) else 2, piece).wait_recv()
    for hop in range(4):
        for piece in range(3):
            for side in range(2):
                if moves(side, hop, piece):
                    copy_of(side, hop, piece).wait_send()


def gather_rows(img_rows, txt_rows, groups):
    return pl.pallas_call(
        functools.partial(gather_kernel, groups),
        out_shape=(
            jax.ShapeDtypeStruct((TP,) + img_rows.shape, img_rows.dtype),
            jax.ShapeDtypeStruct((TP,) + txt_rows.shape, txt_rows.dtype),
        ),
        in_specs=[pl.BlockSpec(memory_space=pltpu.VMEM)] * 2,
        out_specs=(pl.BlockSpec(memory_space=pltpu.VMEM),) * 2,
        scratch_shapes=[pltpu.SemaphoreType.DMA((2, 4, 3)), pltpu.SemaphoreType.DMA((2, 4, 3))],
        compiler_params=pltpu.CompilerParams(collective_id=1, has_side_effects=True),
    )(img_rows, txt_rows)


def scatter_kernel(groups, piece_rows, *refs):
    count = len(piece_rows)
    part_refs = refs[:count]
    out_ref, recv, send, send_sem, recv_sem = refs[count:]
    member, sides = ring_of(groups)
    pieces = []
    row = 0
    for index, sizes in enumerate(piece_rows):
        start = 0
        for size in sizes:
            pieces.append((part_refs[index], start, row, size))
            start += size
            row += size

    def moves(side, hop, piece):
        return hop > 0 or (piece < 2) == (side == 0)

    def dest_of(side, hop):
        return member(4 - hop if side == 0 else hop - 4)

    def copy_of(side, hop, piece):
        part_ref, start, row, size = pieces[piece]
        if hop == 0:
            source = part_ref.at[dest_of(side, hop), pl.ds(start, size)]
        elif moves(side, hop - 1, piece):
            source = send.at[side, hop, pl.ds(row, size)]
        else:
            source = part_ref.at[dest_of(side, hop), pl.ds(start, size)]
        return pltpu.make_async_remote_copy(
            src_ref=source,
            dst_ref=recv.at[side, hop, pl.ds(row, size)],
            send_sem=send_sem.at[side, hop, piece],
            recv_sem=recv_sem.at[side, hop, piece],
            device_id={"dp": sides[side]},
            device_id_type=MESH,
        )

    greet(sides)
    for hop in range(4):
        for piece in range(len(pieces)):
            for side in range(2):
                if moves(side, hop, piece):
                    if hop > 0 and moves(side, hop - 1, piece):
                        part_ref, start, row, size = pieces[piece]
                        copy_of(side, hop - 1, piece).wait_recv()
                        send[side, hop, pl.ds(row, size)] = (
                            recv[side, hop - 1, pl.ds(row, size)].astype(jnp.float32)
                            + part_ref[dest_of(side, hop), pl.ds(start, size)].astype(jnp.float32)
                        ).astype(send.dtype)
                    copy_of(side, hop, piece).start()
    me = member(0)
    for piece in range(len(pieces)):
        part_ref, start, row, size = pieces[piece]
        total = part_ref[me, pl.ds(start, size)].astype(jnp.float32)
        for side in range(2):
            copy_of(side, 3, piece).wait_recv()
            total = total + recv[side, 3, pl.ds(row, size)].astype(jnp.float32)
        out_ref[pl.ds(row, size)] = total
    for hop in range(4):
        for piece in range(len(pieces)):
            for side in range(2):
                if moves(side, hop, piece):
                    copy_of(side, hop, piece).wait_send()


def scatter_sums(parts, piece_rows, groups, collective):
    rows = sum(sum(sizes) for sizes in piece_rows)
    count = sum(len(sizes) for sizes in piece_rows)
    width = parts[0].shape[-1]
    return pl.pallas_call(
        functools.partial(scatter_kernel, groups, piece_rows),
        out_shape=jax.ShapeDtypeStruct((rows, width), jnp.float32),
        in_specs=[pl.BlockSpec(memory_space=pltpu.VMEM)] * len(parts),
        out_specs=pl.BlockSpec(memory_space=pltpu.VMEM),
        scratch_shapes=[
            pltpu.VMEM((2, 4, rows, width), jnp.bfloat16),
            pltpu.VMEM((2, 4, rows, width), jnp.bfloat16),
            pltpu.SemaphoreType.DMA((2, 4, count)),
            pltpu.SemaphoreType.DMA((2, 4, count)),
        ],
        compiler_params=pltpu.CompilerParams(collective_id=collective, has_side_effects=True),
    )(*parts)


def body(
    image_in,
    text_in,
    image_cot,
    text_cot,
    cond_table,
    seq_table,
    text_count,
    mod_weight,
    mod_bias,
    qkv_weight,
    qkv_bias,
    qk_gain,
    out_weight,
    out_bias,
    up_weight,
    up_bias,
    down_weight,
    down_bias,
):
    core = lax.axis_index("section")
    dp_index = lax.axis_index("dp")
    seq_index = lax.axis_index("seq")
    data_parts = lax.axis_size("dp")
    groups = data_parts // TP
    tp_index = dp_index // groups
    group_index = dp_index % groups
    layers = lax.axis_size("section")
    first = core == 0
    batches = image_in.shape[0]
    image_rows = image_in.shape[2]
    text_rows = text_in.shape[2]
    width = image_in.shape[3]
    local_heads = HEADS // TP
    seq_keys = 2 * (image_rows + text_rows)
    key_share = width // TP
    tp_groups = [[t * groups + g for t in range(TP)] for g in range(groups)]
    row_groups = [[t * groups + g for g in range(groups)] for t in range(TP)]
    swap = [(0, 1), (1, 0)]

    def whole_share(value, axis):
        if groups == 1:
            return value
        return lax.all_gather(value, "dp", axis=axis, tiled=True, axis_index_groups=row_groups)

    def across_tp(value, split_axis, concat_axis):
        return lax.all_to_all(
            value, "dp", split_axis, concat_axis, axis_index_groups=tp_groups, tiled=True
        )

    def both_layers(own):
        other = lax.ppermute(own, "section", swap)
        return (jnp.where(first, own, other), jnp.where(first, other, own))

    trade = []
    for d in range(data_parts):
        for s in range(2):
            t, g = (d // groups, d % groups)
            held = (t - t % 2 + s) * groups + g
            trade.append((held * 2 + t % 2, d * 2 + s))

    def to_work(image, text):
        rows = jnp.concatenate(
            [
                lax.dynamic_index_in_dim(image, core, 0, keepdims=False)[0],
                lax.dynamic_index_in_dim(text, core, 0, keepdims=False)[0],
            ],
            axis=0,
        )
        return lax.ppermute(rows, ("dp", "seq"), trade)

    start_rows = to_work(image_in, text_in)

    mod_mats = whole_share(mod_weight[0], 1)
    all_tp = jnp.arange(TP)
    held_tp = all_tp - all_tp % 2 + seq_index
    held_ids = jnp.take(seq_table, held_tp * groups + group_index, axis=0).reshape(-1)
    held_cond = jax.nn.silu(jnp.take(cond_table, held_ids, axis=0).astype(jnp.float32)).astype(
        jnp.bfloat16
    )
    cond_cols = lax.dynamic_slice_in_dim(held_cond, tp_index * key_share, key_share, 1)
    partial_mod = jnp.einsum("rd,sdk->rsk", cond_cols, mod_mats, preferred_element_type=jnp.float32)
    mod_add = whole_share(mod_bias[0], 1).astype(jnp.float32)
    mod_span = mod_add.shape[1]
    mod_cols = partial_mod.shape[2]
    mod_place = lax.dynamic_update_slice(
        jnp.zeros((2, mod_cols), jnp.float32), mod_add, (0, tp_index * mod_span)
    )
    mod_rows_each = batches * 2 * 6
    partial_mod = (partial_mod + mod_place[None]).astype(jnp.bfloat16)
    partial_mod = partial_mod.reshape(TP, mod_rows_each, width)
    own_gain = whole_share(qk_gain[0], 1)
    gain_span = own_gain.shape[1]
    gain_place = lax.dynamic_update_slice(
        jnp.zeros((2, TP * gain_span), jnp.bfloat16), own_gain, (0, tp_index * gain_span)
    ).reshape(-1)
    count_place = lax.dynamic_update_slice(
        jnp.zeros((TP, batches, 2), jnp.bfloat16),
        text_count.transpose(1, 0, 2).astype(jnp.bfloat16),
        (tp_index, 0, 0),
    ).reshape(-1)
    extra = jnp.concatenate([gain_place, count_place])
    extra = jnp.zeros((8, width), jnp.bfloat16).at[0, : extra.shape[0]].set(extra)
    partial_mod = jnp.concatenate(
        [partial_mod, jnp.broadcast_to(extra[None], (TP, 8, width))], axis=1
    )
    mod_sums = scatter_sums((partial_mod,), ((16, 16, 0)[:2],), groups, 3)
    gain_size = 2 * TP * gain_span
    counts = mod_sums[mod_rows_each, gain_size : gain_size + TP * batches * 2].reshape(
        TP, batches, 2
    )
    layer_mods = mod_sums[:mod_rows_each].reshape(batches, 12, width)
    own_pack = jnp.concatenate(
        [
            lax.dynamic_index_in_dim(layer_mods, core, 0, keepdims=False),
            mod_sums[mod_rows_each : mod_rows_each + 1],
        ]
    )
    sent_pack = jnp.concatenate(
        [
            lax.dynamic_index_in_dim(layer_mods, 1 - core, 0, keepdims=False),
            mod_sums[mod_rows_each : mod_rows_each + 1],
        ]
    )
    other_pack = lax.ppermute(sent_pack, "section", swap)
    packs = (
        jnp.where(first, own_pack, other_pack),
        jnp.where(first, other_pack, own_pack),
    )
    mods = tuple(pack[:12].reshape(2, 6, width) for pack in packs)
    gains = tuple(pack[12, :gain_size].reshape(2, 2 * HD) for pack in packs)

    my_counts = lax.dynamic_index_in_dim(counts, core, 1, keepdims=False)
    group_counts = jnp.take_along_axis(
        jnp.take(my_counts, held_tp, axis=0), (all_tp % 2)[:, None], axis=1
    )[:, 0]
    text_pos = jnp.arange(text_rows).astype(jnp.float32)
    text_live = (text_pos[None, :] < group_counts[:, None]).astype(jnp.float32)
    key_mask = jnp.concatenate(
        [jnp.ones((TP, image_rows), jnp.float32), text_live], axis=1
    ).reshape(TP // 2, seq_keys)
    own_live = jnp.concatenate(
        [
            jnp.ones((image_rows,), jnp.float32),
            lax.dynamic_index_in_dim(text_live, tp_index, 0, keepdims=False),
        ]
    )[:, None]

    qkv_mats = both_layers(across_tp(whole_share(qkv_weight[0], 1), 2, 1))
    out_mats = both_layers(whole_share(out_weight[0], 1))
    up_mats = both_layers(across_tp(whole_share(up_weight[0], 1), 2, 1))
    down_mats = both_layers(whole_share(down_weight[0], 1))
    own_adds = [
        whole_share(value[0], 1).astype(jnp.float32)
        for value in (qkv_bias, out_bias, up_bias, down_bias)
    ]
    add_sizes = [value.shape[1] for value in own_adds]
    adds = both_layers(jnp.concatenate(own_adds, axis=1))

    def split_adds(layer):
        parts = []
        start = 0
        for size in add_sizes:
            parts.append(adds[layer][:, start : start + size])
            start += size
        return parts

    def placed(value):
        return lax.dynamic_update_slice(
            jnp.zeros((width,), jnp.float32), value, (tp_index * value.shape[0],)
        )

    def gathered(rows):
        img, txt = gather_rows(rows[:image_rows], rows[image_rows:], groups)
        return (img.reshape(-1, width), txt.reshape(-1, width))

    def scattered(parts):
        half = image_rows // 2
        return scatter_sums(
            (
                parts[0].astype(jnp.bfloat16).reshape(TP, image_rows, width),
                parts[1].astype(jnp.bfloat16).reshape(TP, text_rows, width),
            ),
            ((half, half), (text_rows,)),
            groups,
            2,
        )

    def by_stream(mod_rows, index):
        return jnp.concatenate(
            [
                jnp.broadcast_to(mod_rows[0, index], (image_rows, width)),
                jnp.broadcast_to(mod_rows[1, index], (text_rows, width)),
            ]
        )

    def joined(parts, columns):
        return jnp.concatenate(
            [
                parts[0].reshape(TP, image_rows, columns),
                parts[1].reshape(TP, text_rows, columns),
            ],
            axis=1,
        )

    def parted(value):
        columns = value.shape[-1]
        value = value.reshape(TP, image_rows + text_rows, columns)
        return (
            value[:, :image_rows].reshape(-1, columns),
            value[:, image_rows:].reshape(-1, columns),
        )

    def spread_gain(gain_rows, offset):
        half = jnp.concatenate(
            [
                jnp.broadcast_to(gain_rows[0, offset : offset + HD], (image_rows, HD)),
                jnp.broadcast_to(gain_rows[1, offset : offset + HD], (text_rows, HD)),
            ]
        )
        return jnp.concatenate([half, half])[None, :, None, :]

    def head_inputs(heads, gain_rows):
        query_unit, query_inv = head_norm(heads[:, :, :, 0].astype(jnp.float32))
        key_unit, key_inv = head_norm(heads[:, :, :, 1].astype(jnp.float32))
        query_low = (query_unit * spread_gain(gain_rows, 0)).astype(jnp.bfloat16)
        key_low = (key_unit * spread_gain(gain_rows, HD)).astype(jnp.bfloat16)
        return (query_unit, query_inv, key_unit, key_inv, query_low, key_low)

    def forward(layer, rows):
        mod_rows = mods[layer]
        qkv_add, out_add, up_add, down_add = split_adds(layer)
        values = rows.astype(jnp.float32)
        normed, inv_std = layer_norm(values)
        hidden = (normed * (1.0 + by_stream(mod_rows, 1)) + by_stream(mod_rows, 0)).astype(
            jnp.bfloat16
        )
        hidden_all = gathered(hidden)
        packed = [
            (mat(hidden_all[t], qkv_mats[layer][t]) + qkv_add[t]).astype(jnp.bfloat16)
            for t in range(2)
        ]
        heads = joined(packed, packed[0].shape[-1]).reshape(
            TP // 2, seq_keys, local_heads, 3, HD
        )
        _, _, _, _, query_low, key_low = head_inputs(heads, gains[layer])
        scores = (
            jnp.einsum(
                "bqhd,bkhd->bhqk", query_low, key_low, preferred_element_type=jnp.float32
            )
            * 0.125
        )
        exp_scores = jnp.exp(scores) * key_mask[:, None, None, :]
        denom_sum = jnp.sum(exp_scores, axis=-1, keepdims=True)
        probs_low = (exp_scores / denom_sum).astype(jnp.bfloat16)
        attended = jnp.einsum(
            "bhqk,bkhd->bqhd", probs_low, heads[:, :, :, 2], preferred_element_type=jnp.float32
        ).astype(jnp.bfloat16)
        attended = parted(attended.reshape(TP // 2, seq_keys, local_heads * HD))
        branch = scattered(
            [mat(attended[t], out_mats[layer][t]) + placed(out_add[t]) for t in range(2)]
        )
        middle = values + by_stream(mod_rows, 2) * branch
        normed_mid, inv_mid = layer_norm(middle)
        hidden_mid = (
            normed_mid * (1.0 + by_stream(mod_rows, 4)) + by_stream(mod_rows, 3)
        ).astype(jnp.bfloat16)
        mid_all = gathered(hidden_mid)
        acts = []
        slopes = []
        for t in range(2):
            act_value, act_slope = gelu_both(mat(mid_all[t], up_mats[layer][t]) + up_add[t])
            acts.append(act_value.astype(jnp.bfloat16))
            slopes.append(act_slope)
        mlp_out = scattered(
            [mat(acts[t], down_mats[layer][t]) + placed(down_add[t]) for t in range(2)]
        )
        result = (middle + by_stream(mod_rows, 5) * mlp_out) * own_live
        saved = (
            normed,
            inv_std,
            hidden_all,
            heads,
            denom_sum,
            attended,
            branch,
            normed_mid,
            inv_mid,
            mid_all,
            acts,
            slopes,
            mlp_out,
        )
        return (result.astype(jnp.bfloat16), saved)

    def stream_sums(value):
        return jnp.stack(
            [jnp.sum(value[:image_rows], axis=0), jnp.sum(value[image_rows:], axis=0)]
        )

    def backward(layer, grad_rows, saved):
        (
            normed,
            inv_std,
            hidden_all,
            heads,
            denom_sum,
            attended,
            branch,
            normed_mid,
            inv_mid,
            mid_all,
            acts,
            slopes,
            mlp_out,
        ) = saved
        mod_rows = mods[layer]
        grad_out = grad_rows * own_live
        gate_two = stream_sums(grad_out * mlp_out)
        mlp_all = gathered((by_stream(mod_rows, 5) * grad_out).astype(jnp.bfloat16))
        pre_grads = [
            (back_product(mlp_all[t], down_mats[layer][t]) * slopes[t]).astype(jnp.bfloat16)
            for t in range(2)
        ]
        hidden_grad = scattered([back_product(pre_grads[t], up_mats[layer][t]) for t in range(2)])
        down_grads = [rows_product(acts[t], mlp_all[t]).astype(jnp.bfloat16) for t in range(2)]
        up_grads = [rows_product(mid_all[t], pre_grads[t]).astype(jnp.bfloat16) for t in range(2)]
        scale_two = stream_sums(hidden_grad * normed_mid)
        shift_two = stream_sums(hidden_grad)
        middle_grad = grad_out + norm_back(
            hidden_grad * (1.0 + by_stream(mod_rows, 4)), normed_mid, inv_mid
        )
        gate_one = stream_sums(middle_grad * branch)
        branch_all = gathered((by_stream(mod_rows, 2) * middle_grad).astype(jnp.bfloat16))
        attn_grads = [
            back_product(branch_all[t], out_mats[layer][t]).astype(jnp.bfloat16) for t in range(2)
        ]
        out_grads = [rows_product(attended[t], branch_all[t]).astype(jnp.bfloat16) for t in range(2)]
        out_grad = joined(attn_grads, local_heads * HD).reshape(
            TP // 2, seq_keys, local_heads, HD
        )
        query_unit, query_inv, key_unit, key_inv, query_low, key_low = head_inputs(
            heads, gains[layer]
        )
        scores = (
            jnp.einsum(
                "bqhd,bkhd->bhqk", query_low, key_low, preferred_element_type=jnp.float32
            )
            * 0.125
        )
        probs = jnp.exp(scores) * key_mask[:, None, None, :] / denom_sum
        prob_grad = jnp.einsum(
            "bqhd,bkhd->bhqk", out_grad, heads[:, :, :, 2], preferred_element_type=jnp.float32
        )
        row_dot = jnp.sum(probs * prob_grad, axis=-1, keepdims=True)
        score_grad = (probs * (prob_grad - row_dot)).astype(jnp.bfloat16)
        value_grad = jnp.einsum(
            "bhqk,bqhd->bkhd",
            probs.astype(jnp.bfloat16),
            out_grad,
            preferred_element_type=jnp.float32,
        )
        query_grad = (
            jnp.einsum("bhqk,bkhd->bqhd", score_grad, key_low, preferred_element_type=jnp.float32)
            * 0.125
        )
        key_grad = (
            jnp.einsum("bhqk,bqhd->bkhd", score_grad, query_low, preferred_element_type=jnp.float32)
            * 0.125
        )

        def gain_sums(grad, unit):
            row_sums = jnp.sum(grad * unit, axis=(0, 2)).reshape(2, image_rows + text_rows, HD)
            return jnp.stack(
                [
                    jnp.sum(row_sums[:, :image_rows], axis=(0, 1)),
                    jnp.sum(row_sums[:, image_rows:], axis=(0, 1)),
                ]
            )

        gain_grad = jnp.concatenate(
            [gain_sums(query_grad, query_unit), gain_sums(key_grad, key_unit)], axis=1
        )
        packed_grad = jnp.stack(
            [
                head_back(query_grad * spread_gain(gains[layer], 0), query_unit, query_inv),
                head_back(key_grad * spread_gain(gains[layer], HD), key_unit, key_inv),
                value_grad,
            ],
            axis=3,
        ).astype(jnp.bfloat16)
        qkv_grads = parted(packed_grad.reshape(TP // 2, seq_keys, local_heads * 3 * HD))
        hidden_grad = scattered([back_product(qkv_grads[t], qkv_mats[layer][t]) for t in range(2)])
        weight_grads = [
            rows_product(hidden_all[t], qkv_grads[t]).astype(jnp.bfloat16) for t in range(2)
        ]
        scale_one = stream_sums(hidden_grad * normed)
        shift_one = stream_sums(hidden_grad)
        grad_in = middle_grad + norm_back(
            hidden_grad * (1.0 + by_stream(mod_rows, 1)), normed, inv_std
        )
        mod_grad = jnp.stack(
            [shift_one, scale_one, gate_one, shift_two, scale_two, gate_two], axis=1
        )

        def own_columns(value):
            share = value.shape[1] // TP
            return lax.dynamic_slice_in_dim(value, tp_index * share, share, 1)

        def row_sums(values):
            return jnp.stack([jnp.sum(value.astype(jnp.float32), axis=0) for value in values])

        bias_grads = (
            row_sums(qkv_grads),
            own_columns(row_sums(branch_all)),
            row_sums(pre_grads),
            own_columns(row_sums(mlp_all)),
        )
        return (
            grad_in,
            mod_grad,
            gain_grad,
            bias_grads,
            (
                jnp.stack(weight_grads),
                jnp.stack(out_grads),
                jnp.stack(up_grads),
                jnp.stack(down_grads),
            ),
        )

    def settle(value, by_columns):
        columns = value.shape[-1]
        blocks = TP if by_columns else 1
        value = value.reshape(2, blocks, -1, columns)
        if groups > 1:
            value = lax.psum_scatter(
                value, "dp", scatter_dimension=2, axis_index_groups=row_groups, tiled=True
            )
        half = value.shape[2] // 2
        sent = lax.dynamic_slice_in_dim(value, (1 - core) * half, half, 2)
        kept = lax.dynamic_slice_in_dim(value, core * half, half, 2)
        kept = (
            kept.astype(jnp.float32) + lax.ppermute(sent, "section", swap).astype(jnp.float32)
        ).astype(jnp.bfloat16)
        sent = lax.dynamic_index_in_dim(kept, 1 - seq_index, 0, keepdims=False)
        kept = lax.dynamic_index_in_dim(kept, seq_index, 0, keepdims=False)
        kept = (
            kept.astype(jnp.float32) + lax.ppermute(sent, "seq", swap).astype(jnp.float32)
        ).astype(jnp.bfloat16)
        if by_columns:
            kept = lax.all_to_all(
                kept, "dp", 0, 0, axis_index_groups=tp_groups, tiled=True
            )
            kept = kept.transpose(1, 0, 2).reshape(half, TP * columns)
        else:
            kept = kept[0]
        other = lax.ppermute(kept, "seq", swap)
        return jnp.stack(
            [
                jnp.where(seq_index == 0, kept, other),
                jnp.where(seq_index == 0, other, kept),
            ]
        )

    def owned(early, late):
        other = lax.ppermute(jnp.where(first, late, early), "section", swap)
        return jnp.concatenate(
            [jnp.where(first, early, other), jnp.where(first, other, late)], axis=1
        ).astype(jnp.float32)[None]

    middle_rows, early_saved = forward(0, start_rows)
    final_rows, late_saved = forward(1, middle_rows)
    cot_rows = to_work(image_cot, text_cot).astype(jnp.float32)
    late_in, late_mod, late_gain, late_bias, late_weights = backward(1, cot_rows, late_saved)
    late_low = late_in.astype(jnp.bfloat16)
    late_settled = [settle(late_weights[k], k in (0, 2)) for k in range(4)]
    early_in, early_mod, early_gain, early_bias, early_weights = backward(
        0, late_low.astype(jnp.float32), early_saved
    )
    early_settled = [settle(early_weights[k], k in (0, 2)) for k in range(4)]
    weight_outs = [owned(early_settled[k], late_settled[k]) for k in range(4)]

    def to_owner(early, late):
        other = lax.ppermute(jnp.where(first, late, early), "section", swap)
        both = jnp.stack([jnp.where(first, early, other), jnp.where(first, other, late)])
        return lax.ppermute(both, ("dp", "seq"), trade)

    act_all = to_owner(middle_rows, final_rows)
    grad_all = to_owner(early_in.astype(jnp.bfloat16), late_low).astype(jnp.float32)
    image_out = act_all[:, :image_rows][None, :, None]
    text_out = act_all[:, image_rows:][None, :, None]
    image_grad = grad_all[:, :image_rows][None, :, None]
    text_grad = grad_all[:, image_rows:][None, :, None]

    def bias_total(parts_early, parts_late):
        early = jnp.concatenate(parts_early, axis=1)
        late = jnp.concatenate(parts_late, axis=1)
        own = jnp.where(first, early, late) + lax.ppermute(
            jnp.where(first, late, early), "section", swap
        )
        own = own + lax.ppermute(own, "seq", swap)
        if groups > 1:
            own = lax.psum(own, "dp", axis_index_groups=row_groups)
        outs = []
        start = 0
        for value in parts_early:
            size = value.shape[1]
            share = size // groups
            outs.append(
                lax.dynamic_slice_in_dim(
                    own[:, start : start + size], group_index * share, share, 1
                )[None]
            )
            start += size
        return outs

    bias_outs = bias_total(early_bias, late_bias)

    def mod_pack(mod_grad, gain_grad):
        row = jnp.zeros((1, width), jnp.float32).at[0, : 4 * HD].set(gain_grad.reshape(-1))
        return jnp.concatenate([mod_grad.reshape(12, width), row])

    early_pack = mod_pack(early_mod, early_gain)
    late_pack = mod_pack(late_mod, late_gain)
    own_mod = jnp.where(first, early_pack, late_pack).astype(jnp.bfloat16)
    other_mod = lax.ppermute(
        jnp.where(first, late_pack, early_pack).astype(jnp.bfloat16), "section", swap
    )
    mod_both = jnp.stack([jnp.where(first, own_mod, other_mod), jnp.where(first, other_mod, own_mod)])
    every_mod = lax.all_gather(mod_both, ("dp", "seq"), axis=0, tiled=True)
    every_mod = every_mod.reshape(data_parts, 2, batches, 13, width)
    place = jnp.arange(data_parts)
    place_tp = place // groups
    held_dp = (
        (place_tp - place_tp % 2)[:, None] + jnp.arange(2)[None, :]
    ) * groups + (place % groups)[:, None]
    every_ids = jnp.take(seq_table, held_dp.reshape(-1), axis=0).reshape(-1)
    every_cond = jax.nn.silu(jnp.take(cond_table, every_ids, axis=0).astype(jnp.float32)).astype(
        jnp.bfloat16
    )
    own_share = mod_weight.shape[2]
    every_cols = lax.dynamic_slice_in_dim(every_cond, dp_index * own_share, own_share, 1)
    mod_flat = every_mod[:, :, :, :12].reshape(-1, 2, 6 * width)
    modw_grad = jnp.einsum(
        "rd,rsk->sdk", every_cols, mod_flat, preferred_element_type=jnp.float32
    )[None]
    bias_share = mod_bias.shape[2]
    modb_grad = jnp.sum(
        lax.dynamic_slice_in_dim(mod_flat, dp_index * bias_share, bias_share, 2).astype(
            jnp.float32
        ),
        axis=0,
    )[None]
    gain_total = jnp.sum(every_mod[:, :, :, 12, : 4 * HD].astype(jnp.float32), axis=(0, 1, 2))
    gain_share = qk_gain.shape[2]
    gain_out = lax.dynamic_slice_in_dim(
        gain_total.reshape(2, 2 * HD), dp_index * gain_share, gain_share, 1
    )[None]
    return (
        image_out,
        text_out,
        image_grad,
        text_grad,
        modw_grad,
        modb_grad,
        weight_outs[0],
        bias_outs[0],
        gain_out,
        weight_outs[1],
        bias_outs[1],
        weight_outs[2],
        bias_outs[2],
        weight_outs[3],
        bias_outs[3],
    )


def solution(mesh):
    return jax.shard_map(
        body,
        mesh=mesh,
        in_specs=(
            P(None, "dp", "seq", None),
            P(None, "dp", "seq", None),
            P(None, "dp", "seq", None),
            P(None, "dp", "seq", None),
            P(),
            P(),
            P(None, "dp", None),
            P("section", None, "dp", None),
            P("section", None, "dp"),
            P("section", None, "dp", None),
            P("section", None, "dp"),
            P("section", None, "dp"),
            P("section", None, "dp", None),
            P("section", None, "dp"),
            P("section", None, "dp", None),
            P("section", None, "dp"),
            P("section", None, "dp", None),
            P("section", None, "dp"),
        ),
        out_specs=(
            P("section", None, "dp", "seq", None),
            P("section", None, "dp", "seq", None),
            P("section", None, "dp", "seq", None),
            P("section", None, "dp", "seq", None),
            P("section", None, "dp", None),
            P("section", None, "dp"),
            P("section", None, "dp", None),
            P("section", None, "dp"),
            P("section", None, "dp"),
            P("section", None, "dp", None),
            P("section", None, "dp"),
            P("section", None, "dp", None),
            P("section", None, "dp"),
            P("section", None, "dp", None),
            P("section", None, "dp"),
        ),
        check_vma=False,
    )
```

time: 5720 us -> 1490 us (0.26)
  waiting for transfers between devices: 4440 us -> 202 us
  Pallas kernels: 0 us -> 583 us
  matrix products: 484 us -> 151 us
  blocking collectives: 306 us -> 0 us
  other arithmetic: 87.5 us -> 185 us
    all_gather x5 -> x1, waiting for transfers between devices: 1750 us -> 0.01 us  [body(): every_mod = lax.all_gather(mod_both, ('dp', 'seq'), axis=0, tiled=True)]
    reduce_scatter x8 -> x0, waiting for transfers between devices: 1700 us -> none  [the longest x6 1080 us: settle(): lax.psum_scatter(first_grad.astype(jnp.bfloat16), 'dp', scatter_dimension...]
    unnamed x36 -> x1, waiting for transfers between devices: 632 us -> 0.02 us
    pallas_call x0 -> x17, Pallas kernels: none -> 583 us  [the longest x9 312 us: scatter_sums(): pl.pallas_call(functools.partial(scatter_kernel, groups, piece_rows), out...]
    psum x1 -> x0, waiting for transfers between devices: 309 us -> none  [settle(): lax.psum(owned[0].astype(jnp.bfloat16), 'seq').astype(jnp.float32)]
    all_gather x6 -> x0, blocking collectives: 298 us -> none  [the longest x1 106 us: body(): lax.all_gather(qkv_bias, 'dp', axis=2, tiled=True)]
    ppermute x4 -> x43, waiting for transfers between devices: 1.81 us -> 195 us  [the longest x8 115 us: settle(): other = lax.ppermute(kept, 'seq', swap)]
    dot_general x24 -> x16, matrix products: 210 us -> 52.7 us  [back_product(): lax.dot_general(grad_rows, weight_mat, (((1,), (1,)), ((), ())), preferre...]
  transfers between devices with their start and end apart: 53 -> 50, of which waited for: 35 -> 16; matrix products, arithmetic and copies ran while one was open for 10% -> 21% of each run, Pallas kernels for 0% -> 20%
where the time goes in v1:
time: 1490 us; the launch traced here: 1480 us
  Pallas kernels  583 us (39%)
  local copies, waits for them, and re-layouts  232 us (16%)
  waiting for transfers between devices  202 us (14%)
  other arithmetic  185 us (12%)
  matrix products  151 us (10%)
  starting transfers between devices  105 us (7%)
  between operations  18.9 us (1%)
    pallas_call x9, Pallas kernels, scatter_sums(): pl.pallas_call(functools.partial(scatter_kernel, groups, piece_rows), out...  312 us
    pallas_call x8, Pallas kernels, gather_rows(): pl.pallas_call(functools.partial(gather_kernel, groups), out_shape=(jax.S...  271 us
    ppermute x8, waiting for transfers between devices, settle(): other = lax.ppermute(kept, 'seq', swap)  115 us
    ppermute x8, waiting for transfers between devices, settle(): lax.ppermute(sent, 'seq', swap).astype(jnp.float32)  79.3 us
    unnamed x538, local copies, waits for them, and re-layouts  62.8 us
    dot_general x16, matrix products, back_product(): lax.dot_general(grad_rows, weight_mat, (((1,), (1,)), ((), ())), preferre...  52.7 us
    ppermute x8, starting transfers between devices, settle(): lax.ppermute(sent, 'seq', swap).astype(jnp.float32)  45 us
    dot_general x16, matrix products, mat(): lax.dot_general(left, right, (((1,), (0,)), ((), ())), preferred_element_...  39.1 us
  transfers between devices with their start and end apart: 50, of which 16 were waited for; matrix products, arithmetic and copies ran while one was open for 21% of the time, Pallas kernels for 20%

profile of v1, /device:TPU:0, one launch (start us, length us, event | category | flops | bytes accessed | tf_op | source)
XLA Modules:
  0.0 1476.4 jit_solution(10801241851674574648)
XLA Ops:
  7.2 12.2 copy.177
  19.5 7.4 all-to-all-start
  37.8 104.1 %shard_map.289 = f32[32,1536]{1,0:T(8,128)} custom-call(bf16[8,32,1536]{2,1,0:T(8,128)(2,1)} %pad_maximum_fusion.10.refs_0_), custom_call_target="tpu_custom_call" | custom-call | tf_op jit(solution)/shard_map/pallas_call | solution.py:229
  145.7 15.8 %copy.193 = bf16[1,2,192,6144]{2,1,3,0:T(2,128)(2,1)} copy(bf16[1,2,192,6144]{3,2,1,0:T(8,128)(2,1)} %param.38) | data formatting | bytes 9437184 | tf_op args[14]
  197.5 11.6 copy.178
  209.1 6.2 copy.179
  221.8 108.9 %shard_map.290 = (bf16[8,64,1536]{2,1,0:T(8,128)(2,1)}, bf16[8,32,1536]{2,1,0:T(8,128)(2,1)}) custom-call(bf16[64,1536]{1,0:T(8,128)(2,1)} %slice.718.img_ref, bf16[32,1536]{1,0:T(8,128)(2,1)} %slice.719.txt_ref), custom_call_target="tpu_custom_call" | custom-call | tf_op jit(solution)/shard_map/pallas_call | solution.py:147
  332.3 8.1 broadcast_select_fusion
  340.4 15.7 %copy.253 = bf16[2,192,8,768]{3,1,2,0:T(8,128)(2,1)} copy(bf16[2,192,8,768]{1,0,3,2:T(2,128)(2,1)} %bitcast.52) | data formatting | bytes 9437184 | tf_op jit(solution)/shard_map/all_to_all | solution.py:290
  356.2 5.9 copy.180
  362.2 6.0 broadcast_select_fusion.4
  397.7 28.1 %shard_map.291 = f32[96,1536]{1,0:T(8,128)} custom-call(bf16[8,64,1536]{2,1,0:T(8,128)(2,1)} %bitcast.698, bf16[8,32,1536]{2,1,0:T(8,128)(2,1)} %bitcast.718), custom_call_target="tpu_custom_call" | custom-call | tf_op jit(solution)/shard_map/pallas_call | solution.py:229
  429.9 29.5 %shard_map.292 = (bf16[8,64,1536]{2,1,0:T(8,128)(2,1)}, bf16[8,32,1536]{2,1,0:T(8,128)(2,1)}) custom-call(bf16[64,1536]{1,0:T(8,128)(2,1)} %slice.740.img_ref, bf16[32,1536]{1,0:T(8,128)(2,1)} %slice.741.txt_ref), custom_call_target="tpu_custom_call" | custom-call | tf_op jit(solution)/shard_map/pallas_call | solution.py:147
  459.4 6.7 broadcast_select_fusion.2
  476.0 27.3 %shard_map.293 = f32[96,1536]{1,0:T(8,128)} custom-call(bf16[8,64,1536]{2,1,0:T(8,128)(2,1)} %bitcast.699, bf16[8,32,1536]{2,1,0:T(8,128)(2,1)} %bitcast.722), custom_call_target="tpu_custom_call" | custom-call | tf_op jit(solution)/shard_map/pallas_call | solution.py:229
  508.8 26.4 %shard_map.294 = (bf16[8,64,1536]{2,1,0:T(8,128)(2,1)}, bf16[8,32,1536]{2,1,0:T(8,128)(2,1)}) custom-call(bf16[64,1536]{1,0:T(8,128)(2,1)} %slice.757.img_ref, bf16[32,1536]{1,0:T(8,128)(2,1)} %slice.758.txt_ref), custom_call_target="tpu_custom_call" | custom-call | tf_op jit(solution)/shard_map/pallas_call | solution.py:147
  565.4 24.6 %shard_map.295 = f32[96,1536]{1,0:T(8,128)} custom-call(bf16[8,64,1536]{2,1,0:T(8,128)(2,1)} %bitcast.695, bf16[8,32,1536]{2,1,0:T(8,128)(2,1)} %bitcast.719), custom_call_target="tpu_custom_call" | custom-call | tf_op jit(solution)/shard_map/pallas_call | solution.py:229
  594.9 23.8 %shard_map.296 = (bf16[8,64,1536]{2,1,0:T(8,128)(2,1)}, bf16[8,32,1536]{2,1,0:T(8,128)(2,1)}) custom-call(bf16[64,1536]{1,0:T(8,128)(2,1)} %slice.779.img_ref, bf16[32,1536]{1,0:T(8,128)(2,1)} %slice.780.txt_ref), custom_call_target="tpu_custom_call" | custom-call | tf_op jit(solution)/shard_map/pallas_call | solution.py:147
  631.8 26.7 %shard_map.297 = f32[96,1536]{1,0:T(8,128)} custom-call(bf16[8,64,1536]{2,1,0:T(8,128)(2,1)} %bitcast.700, bf16[8,32,1536]{2,1,0:T(8,128)(2,1)} %bitcast.723), custom_call_target="tpu_custom_call" | custom-call | tf_op jit(solution)/shard_map/pallas_call | solution.py:229
  660.6 20.3 %shard_map.298 = (bf16[8,64,1536]{2,1,0:T(8,128)(2,1)}, bf16[8,32,1536]{2,1,0:T(8,128)(2,1)}) custom-call(bf16[64,1536]{1,0:T(8,128)(2,1)} %slice.791.img_ref, bf16[32,1536]{1,0:T(8,128)(2,1)} %slice.792.txt_ref), custom_call_target="tpu_custom_call" | custom-call | tf_op jit(solution)/shard_map/pallas_call | solution.py:147
  680.8 5.2 convert_reduce_fusion.5
  697.8 26.5 %shard_map.299 = f32[96,1536]{1,0:T(8,128)} custom-call(bf16[8,64,1536]{2,1,0:T(8,128)(2,1)} %bitcast.693, bf16[8,32,1536]{2,1,0:T(8,128)(2,1)} %bitcast.724), custom_call_target="tpu_custom_call" | custom-call | tf_op jit(solution)/shard_map/pallas_call | solution.py:229
  730.7 20.6 %shard_map.300 = (bf16[8,64,1536]{2,1,0:T(8,128)(2,1)}, bf16[8,32,1536]{2,1,0:T(8,128)(2,1)}) custom-call(bf16[64,1536]{1,0:T(8,128)(2,1)} %slice.793.img_ref, bf16[32,1536]{1,0:T(8,128)(2,1)} %slice.794.txt_ref), custom_call_target="tpu_custom_call" | custom-call | tf_op jit(solution)/shard_map/pallas_call | solution.py:147
  776.1 28.7 %shard_map.301 = f32[96,1536]{1,0:T(8,128)} custom-call(bf16[8,64,1536]{2,1,0:T(8,128)(2,1)} %bitcast.696, bf16[8,32,1536]{2,1,0:T(8,128)(2,1)} %bitcast.720), custom_call_target="tpu_custom_call" | custom-call | tf_op jit(solution)/shard_map/pallas_call | solution.py:229
  810.5 21.3 %shard_map.302 = (bf16[8,64,1536]{2,1,0:T(8,128)(2,1)}, bf16[8,32,1536]{2,1,0:T(8,128)(2,1)}) custom-call(bf16[64,1536]{1,0:T(8,128)(2,1)} %slice.797.img_ref, bf16[32,1536]{1,0:T(8,128)(2,1)} %slice.798.txt_ref), custom_call_target="tpu_custom_call" | custom-call | tf_op jit(solution)/shard_map/pallas_call | solution.py:147
  831.8 5.2 convert_reduce_fusion.8
  849.0 25.2 %shard_map.303 = f32[96,1536]{1,0:T(8,128)} custom-call(bf16[8,64,1536]{2,1,0:T(8,128)(2,1)} %bitcast.694, bf16[8,32,1536]{2,1,0:T(8,128)(2,1)} %bitcast.725), custom_call_target="tpu_custom_call" | custom-call | tf_op jit(solution)/shard_map/pallas_call | solution.py:229
  879.3 20.5 %shard_map.304 = (bf16[8,64,1536]{2,1,0:T(8,128)(2,1)}, bf16[8,32,1536]{2,1,0:T(8,128)(2,1)}) custom-call(bf16[64,1536]{1,0:T(8,128)(2,1)} %slice.799.img_ref, bf16[32,1536]{1,0:T(8,128)(2,1)} %slice.800.txt_ref), custom_call_target="tpu_custom_call" | custom-call | tf_op jit(solution)/shard_map/pallas_call | solution.py:147
  930.4 20.5 %shard_map.305 = f32[96,1536]{1,0:T(8,128)} custom-call(bf16[8,64,1536]{2,1,0:T(8,128)(2,1)} %bitcast.697, bf16[8,32,1536]{2,1,0:T(8,128)(2,1)} %bitcast.721), custom_call_target="tpu_custom_call" | custom-call | tf_op jit(solution)/shard_map/pallas_call | solution.py:229
  1083.2 18.8 %collective-permute-start.26 = (bf16[1,96,1536]{2,1,0:T(8,128)(2,1)S(1)}, bf16[1,96,1536]{2,1,0:T(8,128)(2,1)S(1)}, u32[]{:S(2)}, u32[]{:S(2)}) collective-permute-start(bf16[1,96,1536]{2,1,0:T(8,128)(2,1)S(1)} %dynamic-slice_bitcast_fusion.6), channel_id=1, source_target_pairs={{0,1},{1,0},{2,3},{3,2},{4,5},{5,4},{6,7},{7,6},{8,9},{9,8},{10,11... | collective-permute-start | bytes 884744 | tf_op jit(solution)/shard_map/ppermute | solution.py:692
  1103.8 5.2 collective-permute-done.26
  1110.9 7.8 collective-permute-done.23
  1120.3 6.0 collective-permute-done.27
  1127.5 10.1 collective-permute-done.24
  1146.1 19.5 %collective-permute-start.17 = (bf16[8,96,576]{2,1,0:T(8,128)(2,1)S(1)}, bf16[8,96,576]{2,1,0:T(8,128)(2,1)S(1)}, u32[]{:S(2)}, u32[]{:S(2)}) collective-permute-start(bf16[8,96,576]{2,1,0:T(8,128)(2,1)S(1)} %dynamic-slice_bitcast_fusion.4), channel_id=1, source_target_pairs={{0,1},{1,0},{2,3},{3,2},{4,5},{5,4},{6,7},{7,6},{8,9},{9,8},{10,11... | collective-permute-start | bytes 2654216 | tf_op jit(solution)/shard_map/ppermute | solution.py:692
  1176.7 11.6 collective-permute-done.17
  1189.5 6.0 all-to-all-start.3
  1211.8 7.5 all-to-all-done.3
  1226.9 33.0 %collective-permute-done.40 = bf16[1,384,1536]{2,1,0:T(8,128)(2,1)} collective-permute-done((bf16[1,384,1536]{2,1,0:T(8,128)(2,1)}, bf16[1,384,1536]{2,1,0:T(8,128)(2,1)}, u32[]{:S(2)}, u32[]{:S(2)}) %collective-permute-start.40) | collective-permute-done | bytes 1179680 | tf_op jit(solution)/shard_map/ppermute | solution.py:692
  1264.9 20.3 %collective-permute-done.37 = bf16[1,384,1536]{2,1,0:T(8,128)(2,1)} collective-permute-done((bf16[1,384,1536]{2,1,0:T(8,128)(2,1)}, bf16[1,384,1536]{2,1,0:T(8,128)(2,1)}, u32[]{:S(2)}, u32[]{:S(2)}) %collective-permute-start.37) | collective-permute-done | bytes 1179680 | tf_op jit(solution)/shard_map/ppermute | solution.py:692
  1303.7 8.7 convolution_bitcast_fusion
  1323.2 12.6 collective-permute-done.41
  1337.6 23.5 %collective-permute-done.38 = bf16[384,1536]{1,0:T(8,128)(2,1)} collective-permute-done((bf16[384,1536]{1,0:T(8,128)(2,1)}, bf16[384,1536]{1,0:T(8,128)(2,1)}, u32[]{:S(2)}, u32[]{:S(2)}) %collective-permute-start.38) | collective-permute-done | bytes 1179680 | tf_op jit(solution)/shard_map/ppermute | solution.py:701
  1365.0 6.2 all-to-all-start.4
  1371.2 8.8 collective-permute-done.18
  1386.6 12.3 collective-permute-done.15
  1405.8 18.4 %collective-permute-done.34 = bf16[96,6144]{1,0:T(8,128)(2,1)} collective-permute-done((bf16[96,6144]{1,0:T(8,128)(2,1)}, bf16[96,6144]{1,0:T(8,128)(2,1)}, u32[]{:S(2)}, u32[]{:S(2)}) %collective-permute-start.34) | collective-permute-done | bytes 1179680 | tf_op jit(solution)/shard_map/ppermute | solution.py:701
  1426.0 23.1 %collective-permute-done.31 = bf16[96,6144]{1,0:T(8,128)(2,1)S(1)} collective-permute-done((bf16[96,6144]{1,0:T(8,128)(2,1)S(1)}, bf16[96,6144]{1,0:T(8,128)(2,1)S(1)}, u32[]{:S(2)}, u32[]{:S(2)}) %collective-permute-start.31) | collective-permute-done | bytes 1179680 | tf_op jit(solution)/shard_map/ppermute | solution.py:701
  (1137 shorter events, 509.0 us)
Async XLA Ops:
  19.5 142.8 %all-to-all-start = ((bf16[2,192,4608]{1,0,2:T(2,128)(2,1)}), bf16[2,192,4608]{1,0,2:T(2,128)(2,1)}, u32[]{:S(2)}, u32[]{:S(2)}) async-start(bf16[2,192,4608]{1,0,2:T(2,128)(2,1)} %bitcast.662), calls=%async_computation | async-start | bytes 9437184 | tf_op jit(solution)/shard_map/all_to_all | solution.py:290
  27.7 191.2 %collective-permute-start = (bf16[96,1536]{1,0:T(8,128)(2,1)}, bf16[96,1536]{1,0:T(8,128)(2,1)S(1)}, u32[]{:S(2)}, u32[]{:S(2)}) collective-permute-start(bf16[96,1536]{1,0:T(8,128)(2,1)} %pad_maximum_fusion.21), channel_id=1, source_target_pairs={{0,0},{2,1},{1,2},{3,3},{4,4},{6,5},{5,6},{7,7},{8,8},{10,9},{9,10... | collective-permute-start | bytes 884744 | tf_op jit(solution)/shard_map/ppermute | solution.py:313
  143.7 52.0 %collective-permute-start.1 = (f32[13,1536]{1,0:T(8,128)S(1)}, f32[13,1536]{1,0:T(8,128)S(1)}, u32[]{:S(2)}, u32[]{:S(2)}) collective-permute-start(f32[13,1536]{1,0:T(8,128)S(1)} %pad_maximum_fusion.23), channel_id=1, source_target_pairs={{0,16},{16,0},{1,17},{17,1},{2,18},{18,2},{3,19},{19,3},{4,20},{20... | collective-permute-start | bytes 239624 | tf_op jit(solution)/shard_map/ppermute | solution.py:368
  144.0 30.1 %collective-permute-start.3 = (f32[2,1728]{1,0:T(2,128)S(1)}, f32[2,1728]{1,0:T(2,128)S(1)}, u32[]{:S(2)}, u32[]{:S(2)}) collective-permute-start(f32[2,1728]{1,0:T(2,128)S(1)} %concatenate.223), channel_id=1, source_target_pairs={{0,16},{16,0},{1,17},{17,1},{2,18},{18,2},{3,19},{19,3},{4,20},{20... | collective-permute-start | bytes 41480 | tf_op jit(solution)/shard_map/ppermute | solution.py:295
  144.4 186.2 %collective-permute-start.4 = (bf16[2,192,1536]{2,1,0:T(8,128)(2,1)S(1)}, bf16[2,192,1536]{2,1,0:T(8,128)(2,1)S(1)}, u32[]{:S(2)}, u32[]{:S(2)}) collective-permute-start(bf16[2,192,1536]{2,1,0:T(8,128)(2,1)S(1)} %bitcast.703), channel_id=1, source_target_pairs={{0,16},{16,0},{1,17},{17,1},{2,18},{18,2},{3,19},{19,3},{4,20},{20... | collective-permute-start | bytes 3538952 | tf_op jit(solution)/shard_map/ppermute | solution.py:295
  144.5 187.8 %collective-permute-start.6 = (bf16[2,768,1536]{2,1,0:T(8,128)(2,1)}, bf16[2,768,1536]{2,1,0:T(8,128)(2,1)}, u32[]{:S(2)}, u32[]{:S(2)}) collective-permute-start(bf16[2,768,1536]{2,1,0:T(8,128)(2,1)} %bitcast.678), channel_id=1, source_target_pairs={{0,16},{16,0},{1,17},{17,1},{2,18},{18,2},{3,19},{19,3},{4,20},{20... | collective-permute-start | bytes 14155784 | tf_op jit(solution)/shard_map/ppermute | solution.py:295
  162.3 178.1 %all-to-all-start.1 = ((bf16[2,192,6144]{1,0,2:T(2,128)(2,1)}), bf16[2,192,6144]{1,0,2:T(2,128)(2,1)}, u32[]{:S(2)}, u32[]{:S(2)}) async-start(bf16[2,192,6144]{1,0,2:T(2,128)(2,1)} %bitcast.657), calls=%async_computation.1 | async-start | bytes 12582912 | tf_op jit(solution)/shard_map/all_to_all | solution.py:290
  167.1 1058.7 %all-gather.2.cloned.1.call-start = ((), (), s32[]{:S(2)}) async-start(), calls=%async_computation.6 | async-start | bytes 1671168 | tf_op jit(solution)/shard_map/all_gather | solution.py:774
  174.1 329.3 %collective-permute-start.9 = (bf16[96,1536]{1,0:T(8,128)(2,1)}, bf16[96,1536]{1,0:T(8,128)(2,1)}, u32[]{:S(2)}, u32[]{:S(2)}) collective-permute-start(bf16[96,1536]{1,0:T(8,128)(2,1)} %pad_maximum_fusion.22), channel_id=1, source_target_pairs={{0,0},{2,1},{1,2},{3,3},{4,4},{6,5},{5,6},{7,7},{8,8},{10,9},{9,10... | collective-permute-start | bytes 884744 | tf_op jit(solution)/shard_map/ppermute | solution.py:313
  215.2 141.0 %collective-permute-start.2 = (bf16[2,1536,576]{1,2,0:T(8,128)(2,1)}, bf16[2,1536,576]{1,2,0:T(8,128)(2,1)}, u32[]{:S(2)}, u32[]{:S(2)}) collective-permute-start(bf16[2,1536,576]{1,2,0:T(8,128)(2,1)} %copy.179), channel_id=1, source_target_pairs={{0,16},{16,0},{1,17},{17,1},{2,18},{18,2},{3,19},{19,3},{4,20},{20... | collective-permute-start | bytes 10616840 | tf_op jit(solution)/shard_map/ppermute | solution.py:295
  356.2 103.2 %collective-permute-start.5 = (bf16[2,1536,768]{2,1,0:T(8,128)(2,1)}, bf16[2,1536,768]{2,1,0:T(8,128)(2,1)}, u32[]{:S(2)}, u32[]{:S(2)}) collective-permute-start(bf16[2,1536,768]{2,1,0:T(8,128)(2,1)} %bitcast.663), channel_id=1, source_target_pairs={{0,16},{16,0},{1,17},{17,1},{2,18},{18,2},{3,19},{19,3},{4,20},{20... | collective-permute-start | bytes 14155784 | tf_op jit(solution)/shard_map/ppermute | solution.py:295
  1020.8 56.8 %collective-permute-start.7 = (bf16[96,1536]{1,0:T(8,128)(2,1)}, bf16[96,1536]{1,0:T(8,128)(2,1)}, u32[]{:S(2)}, u32[]{:S(2)}) collective-permute-start(bf16[96,1536]{1,0:T(8,128)(2,1)} %get-tuple-element.201), channel_id=1, source_target_pairs={{0,16},{16,0},{1,17},{17,1},{2,18},{18,2},{3,19},{19,3},{4,20},{20... | collective-permute-start | bytes 884744 | tf_op jit(solution)/shard_map/ppermute | solution.py:728
  1022.2 56.7 %collective-permute-start.10 = (bf16[96,1536]{1,0:T(8,128)(2,1)}, bf16[96,1536]{1,0:T(8,128)(2,1)}, u32[]{:S(2)}, u32[]{:S(2)}) collective-permute-start(bf16[96,1536]{1,0:T(8,128)(2,1)} %get-tuple-element.199), channel_id=1, source_target_pairs={{0,16},{16,0},{1,17},{17,1},{2,18},{18,2},{3,19},{19,3},{4,20},{20... | collective-permute-start | bytes 884744 | tf_op jit(solution)/shard_map/ppermute | solution.py:728
  1034.7 41.8 %collective-permute-start.12 = (bf16[13,1536]{1,0:T(8,128)(2,1)S(1)}, bf16[13,1536]{1,0:T(8,128)(2,1)S(1)}, u32[]{:S(2)}, u32[]{:S(2)}) collective-permute-start(bf16[13,1536]{1,0:T(8,128)(2,1)S(1)} %select_convert_fusion.1), channel_id=1, source_target_pairs={{0,16},{16,0},{1,17},{17,1},{2,18},{18,2},{3,19},{19,3},{4,20},{20... | collective-permute-start | bytes 119816 | tf_op jit(solution)/shard_map/ppermute | solution.py:770
  1045.9 96.6 %collective-permute-start.16 = (bf16[2,8,96,576]{3,2,1,0:T(8,128)(2,1)}, bf16[2,8,96,576]{3,2,1,0:T(8,128)(2,1)}, u32[]{:S(2)}, u32[]{:S(2)}) collective-permute-start(bf16[2,8,96,576]{3,2,1,0:T(8,128)(2,1)} %fusion.48), channel_id=1, source_target_pairs={{0,16},{16,0},{1,17},{17,1},{2,18},{18,2},{3,19},{19,3},{4,20},{20... | collective-permute-start | bytes 5308424 | tf_op jit(solution)/shard_map/ppermute | solution.py:687
  1047.3 22.4 %collective-permute-start.20 = (f32[2,1728]{1,0:T(2,128)S(1)}, f32[2,1728]{1,0:T(2,128)S(1)}, u32[]{:S(2)}, u32[]{:S(2)}) collective-permute-start(f32[2,1728]{1,0:T(2,128)S(1)} %broadcast_select_fusion.14), channel_id=1, source_target_pairs={{0,16},{16,0},{1,17},{17,1},{2,18},{18,2},{3,19},{19,3},{4,20},{20... | collective-permute-start | bytes 41480 | tf_op jit(solution)/shard_map/ppermute | solution.py:742
  1069.7 4.7 collective-permute-start.21
  1074.4 71.6 %collective-permute-start.13 = (bf16[2,8,96,576]{3,2,1,0:T(8,128)(2,1)}, bf16[2,8,96,576]{3,2,1,0:T(8,128)(2,1)}, u32[]{:S(2)}, u32[]{:S(2)}) collective-permute-start(bf16[2,8,96,576]{3,2,1,0:T(8,128)(2,1)} %fusion.50), channel_id=1, source_target_pairs={{0,16},{16,0},{1,17},{17,1},{2,18},{18,2},{3,19},{19,3},{4,20},{20... | collective-permute-start | bytes 5308424 | tf_op jit(solution)/shard_map/ppermute | solution.py:687
  1076.5 4.2 collective-permute-start.25
  1077.5 4.6 collective-permute-start.22
  1078.9 90.1 %collective-permute-start.32 = (bf16[2,8,96,768]{3,2,1,0:T(8,128)(2,1)}, bf16[2,8,96,768]{3,2,1,0:T(8,128)(2,1)S(1)}, u32[]{:S(2)}, u32[]{:S(2)}) collective-permute-start(bf16[2,8,96,768]{3,2,1,0:T(8,128)(2,1)} %fusion.32), channel_id=1, source_target_pairs={{0,16},{16,0},{1,17},{17,1},{2,18},{18,2},{3,19},{19,3},{4,20},{20... | collective-permute-start | bytes 7077896 | tf_op jit(solution)/shard_map/ppermute | solution.py:687
  1080.7 91.9 %collective-permute-start.39 = (bf16[2,1,384,1536]{3,2,1,0:T(8,128)(2,1)S(1)}, bf16[2,1,384,1536]{3,2,1,0:T(8,128)(2,1)S(1)}, u32[]{:S(2)}, u32[]{:S(2)}) collective-permute-start(bf16[2,1,384,1536]{3,2,1,0:T(8,128)(2,1)S(1)} %copy-done.84), channel_id=1, source_target_pairs={{0,16},{16,0},{1,17},{17,1},{2,18},{18,2},{3,19},{19,3},{4,20},{20... | collective-permute-start | bytes 7077896 | tf_op jit(solution)/shard_map/ppermute | solution.py:687
  1083.2 25.9 %collective-permute-start.26 = (bf16[1,96,1536]{2,1,0:T(8,128)(2,1)S(1)}, bf16[1,96,1536]{2,1,0:T(8,128)(2,1)S(1)}, u32[]{:S(2)}, u32[]{:S(2)}) collective-permute-start(bf16[1,96,1536]{2,1,0:T(8,128)(2,1)S(1)} %dynamic-slice_bitcast_fusion.6), channel_id=1, source_target_pairs={{0,1},{1,0},{2,3},{3,2},{4,5},{5,4},{6,7},{7,6},{8,9},{9,8},{10,11... | collective-permute-start | bytes 884744 | tf_op jit(solution)/shard_map/ppermute | solution.py:692
  1109.1 9.7 collective-permute-start.23
  1118.7 7.5 collective-permute-start.27
  1126.2 11.3 collective-permute-start.24
  1138.4 2.1 collective-permute-start.28
  1140.5 63.2 %collective-permute-start.29 = (bf16[2,8,96,768]{3,2,1,0:T(8,128)(2,1)}, bf16[2,8,96,768]{3,2,1,0:T(8,128)(2,1)}, u32[]{:S(2)}, u32[]{:S(2)}) collective-permute-start(bf16[2,8,96,768]{3,2,1,0:T(8,128)(2,1)} %fusion.34), channel_id=1, source_target_pairs={{0,16},{16,0},{1,17},{17,1},{2,18},{18,2},{3,19},{19,3},{4,20},{20... | collective-permute-start | bytes 7077896 | tf_op jit(solution)/shard_map/ppermute | solution.py:687
  1142.5 56.3 %collective-permute-start.36 = (bf16[2,1,384,1536]{3,2,0,1:T(8,128)(2,1)}, bf16[2,1,384,1536]{3,2,0,1:T(8,128)(2,1)}, u32[]{:S(2)}, u32[]{:S(2)}) collective-permute-start(bf16[2,1,384,1536]{3,2,0,1:T(8,128)(2,1)} %fusion.29), channel_id=1, source_target_pairs={{0,16},{16,0},{1,17},{17,1},{2,18},{18,2},{3,19},{19,3},{4,20},{20... | collective-permute-start | bytes 7077896 | tf_op jit(solution)/shard_map/ppermute | solution.py:687
  1146.1 42.1 %collective-permute-start.17 = (bf16[8,96,576]{2,1,0:T(8,128)(2,1)S(1)}, bf16[8,96,576]{2,1,0:T(8,128)(2,1)S(1)}, u32[]{:S(2)}, u32[]{:S(2)}) collective-permute-start(bf16[8,96,576]{2,1,0:T(8,128)(2,1)S(1)} %dynamic-slice_bitcast_fusion.4), channel_id=1, source_target_pairs={{0,1},{1,0},{2,3},{3,2},{4,5},{5,4},{6,7},{7,6},{8,9},{9,8},{10,11... | collective-permute-start | bytes 2654216 | tf_op jit(solution)/shard_map/ppermute | solution.py:692
  1169.5 39.9 %collective-permute-start.14 = (bf16[8,96,576]{2,1,0:T(8,128)(2,1)}, bf16[8,96,576]{2,1,0:T(8,128)(2,1)}, u32[]{:S(2)}, u32[]{:S(2)}) collective-permute-start(bf16[8,96,576]{2,1,0:T(8,128)(2,1)} %dynamic-slice_bitcast_fusion.5), channel_id=1, source_target_pairs={{0,1},{1,0},{2,3},{3,2},{4,5},{5,4},{6,7},{7,6},{8,9},{9,8},{10,11... | collective-permute-start | bytes 2654216 | tf_op jit(solution)/shard_map/ppermute | solution.py:692
  1172.7 117.2 %collective-permute-start.33 = (bf16[8,96,768]{2,1,0:T(8,128)(2,1)}, bf16[8,96,768]{2,1,0:T(8,128)(2,1)}, u32[]{:S(2)}, u32[]{:S(2)}) collective-permute-start(bf16[8,96,768]{2,1,0:T(8,128)(2,1)} %dynamic-slice_bitcast_fusion.2), channel_id=1, source_target_pairs={{0,1},{1,0},{2,3},{3,2},{4,5},{5,4},{6,7},{7,6},{8,9},{9,8},{10,11... | collective-permute-start | bytes 3538952 | tf_op jit(solution)/shard_map/ppermute | solution.py:692
  1189.5 29.8 %all-to-all-start.3 = ((bf16[8,96,576]{2,1,0:T(8,128)(2,1)}), bf16[8,96,576]{2,1,0:T(8,128)(2,1)}, u32[]{:S(2)}, u32[]{:S(2)}) async-start(bf16[8,96,576]{2,1,0:T(8,128)(2,1)} %fusion.52), calls=%async_computation.3 | async-start | bytes 1966080 | tf_op jit(solution)/shard_map/all_to_all | solution.py:695
  1198.0 61.9 %collective-permute-start.40 = (bf16[1,384,1536]{2,1,0:T(8,128)(2,1)}, bf16[1,384,1536]{2,1,0:T(8,128)(2,1)}, u32[]{:S(2)}, u32[]{:S(2)}) collective-permute-start(bf16[1,384,1536]{2,1,0:T(8,128)(2,1)} %dynamic-slice_bitcast_fusion), channel_id=1, source_target_pairs={{0,1},{1,0},{2,3},{3,2},{4,5},{5,4},{6,7},{7,6},{8,9},{9,8},{10,11... | collective-permute-start | bytes 3538952 | tf_op jit(solution)/shard_map/ppermute | solution.py:692
  1202.5 82.7 %collective-permute-start.37 = (bf16[1,384,1536]{2,1,0:T(8,128)(2,1)}, bf16[1,384,1536]{2,1,0:T(8,128)(2,1)}, u32[]{:S(2)}, u32[]{:S(2)}) collective-permute-start(bf16[1,384,1536]{2,1,0:T(8,128)(2,1)} %dynamic-slice_bitcast_fusion.1), channel_id=1, source_target_pairs={{0,1},{1,0},{2,3},{3,2},{4,5},{5,4},{6,7},{7,6},{8,9},{9,8},{10,11... | collective-permute-start | bytes 3538952 | tf_op jit(solution)/shard_map/ppermute | solution.py:692
  1219.3 73.2 %all-to-all-start.2 = ((bf16[8,96,576]{2,1,0:T(8,128)(2,1)}), bf16[8,96,576]{2,1,0:T(8,128)(2,1)}, u32[]{:S(2)}, u32[]{:S(2)}) async-start(bf16[8,96,576]{2,1,0:T(8,128)(2,1)} %fusion.53), calls=%async_computation.2 | async-start | bytes 1966080 | tf_op jit(solution)/shard_map/all_to_all | solution.py:695
  1225.0 87.3 %collective-permute-start.30 = (bf16[8,96,768]{2,1,0:T(8,128)(2,1)}, bf16[8,96,768]{2,1,0:T(8,128)(2,1)}, u32[]{:S(2)}, u32[]{:S(2)}) collective-permute-start(bf16[8,96,768]{2,1,0:T(8,128)(2,1)} %dynamic-slice_bitcast_fusion.3), channel_id=1, source_target_pairs={{0,1},{1,0},{2,3},{3,2},{4,5},{5,4},{6,7},{7,6},{8,9},{9,8},{10,11... | collective-permute-start | bytes 3538952 | tf_op jit(solution)/shard_map/ppermute | solution.py:692
  1262.9 72.9 %collective-permute-start.41 = (bf16[384,1536]{1,0:T(8,128)(2,1)}, bf16[384,1536]{1,0:T(8,128)(2,1)}, u32[]{:S(2)}, u32[]{:S(2)}) collective-permute-start(bf16[384,1536]{1,0:T(8,128)(2,1)} %fusion.97), channel_id=1, source_target_pairs={{0,1},{1,0},{2,3},{3,2},{4,5},{5,4},{6,7},{7,6},{8,9},{9,8},{10,11... | collective-permute-start | bytes 3538952 | tf_op jit(solution)/shard_map/ppermute | solution.py:701
  1287.8 73.2 %collective-permute-start.38 = (bf16[384,1536]{1,0:T(8,128)(2,1)}, bf16[384,1536]{1,0:T(8,128)(2,1)}, u32[]{:S(2)}, u32[]{:S(2)}) collective-permute-start(bf16[384,1536]{1,0:T(8,128)(2,1)} %fusion.96), channel_id=1, source_target_pairs={{0,1},{1,0},{2,3},{3,2},{4,5},{5,4},{6,7},{7,6},{8,9},{9,8},{10,11... | collective-permute-start | bytes 3538952 | tf_op jit(solution)/shard_map/ppermute | solution.py:701
  1292.4 72.6 %all-to-all-start.5 = ((bf16[8,96,768]{2,1,0:T(8,128)(2,1)}), bf16[8,96,768]{2,1,0:T(8,128)(2,1)}, u32[]{:S(2)}, u32[]{:S(2)}) async-start(bf16[8,96,768]{2,1,0:T(8,128)(2,1)} %fusion.38), calls=%async_computation.5 | async-start | bytes 2359296 | tf_op jit(solution)/shard_map/all_to_all | solution.py:695
  1318.0 62.0 %collective-permute-start.18 = (bf16[96,4608]{1,0:T(8,128)(2,1)}, bf16[96,4608]{1,0:T(8,128)(2,1)}, u32[]{:S(2)}, u32[]{:S(2)}) collective-permute-start(bf16[96,4608]{1,0:T(8,128)(2,1)} %reshape.1118), channel_id=1, source_target_pairs={{0,1},{1,0},{2,3},{3,2},{4,5},{5,4},{6,7},{7,6},{8,9},{9,8},{10,11... | collective-permute-start | bytes 2654216 | tf_op jit(solution)/shard_map/ppermute | solution.py:701
  1322.4 76.6 %collective-permute-start.15 = (bf16[96,4608]{1,0:T(8,128)(2,1)}, bf16[96,4608]{1,0:T(8,128)(2,1)}, u32[]{:S(2)}, u32[]{:S(2)}) collective-permute-start(bf16[96,4608]{1,0:T(8,128)(2,1)} %reshape.1117), channel_id=1, source_target_pairs={{0,1},{1,0},{2,3},{3,2},{4,5},{5,4},{6,7},{7,6},{8,9},{9,8},{10,11... | collective-permute-start | bytes 2654216 | tf_op jit(solution)/shard_map/ppermute | solution.py:701
  1365.0 92.0 %collective-permute-start.42 = (bf16[2,384,1536]{2,1,0:T(8,128)(2,1)}, bf16[2,384,1536]{2,1,0:T(8,128)(2,1)}, u32[]{:S(2)}, u32[]{:S(2)}) collective-permute-start(bf16[2,384,1536]{2,1,0:T(8,128)(2,1)} %broadcast_select_fusion.6), channel_id=1, source_target_pairs={{0,16},{16,0},{1,17},{17,1},{2,18},{18,2},{3,19},{19,3},{4,20},{20... | collective-permute-start | bytes 7077896 | tf_op jit(solution)/shard_map/ppermute | solution.py:710
  1365.0 37.3 %all-to-all-start.4 = ((bf16[8,96,768]{2,1,0:T(8,128)(2,1)}), bf16[8,96,768]{2,1,0:T(8,128)(2,1)}, u32[]{:S(2)}, u32[]{:S(2)}) async-start(bf16[8,96,768]{2,1,0:T(8,128)(2,1)} %fusion.39), calls=%async_computation.4 | async-start | bytes 2359296 | tf_op jit(solution)/shard_map/all_to_all | solution.py:695
  1384.6 39.6 %collective-permute-start.34 = (bf16[96,6144]{1,0:T(8,128)(2,1)}, bf16[96,6144]{1,0:T(8,128)(2,1)}, u32[]{:S(2)}, u32[]{:S(2)}) collective-permute-start(bf16[96,6144]{1,0:T(8,128)(2,1)} %bitcast.282), channel_id=1, source_target_pairs={{0,1},{1,0},{2,3},{3,2},{4,5},{5,4},{6,7},{7,6},{8,9},{9,8},{10,11... | collective-permute-start | bytes 3538952 | tf_op jit(solution)/shard_map/ppermute | solution.py:701
  1402.3 47.5 %collective-permute-start.19 = (bf16[2,96,4608]{2,1,0:T(8,128)(2,1)}, bf16[2,96,4608]{2,1,0:T(8,128)(2,1)}, u32[]{:S(2)}, u32[]{:S(2)}) collective-permute-start(bf16[2,96,4608]{2,1,0:T(8,128)(2,1)} %broadcast_select_fusion.8), channel_id=1, source_target_pairs={{0,16},{16,0},{1,17},{17,1},{2,18},{18,2},{3,19},{19,3},{4,20},{20... | collective-permute-start | bytes 5308424 | tf_op jit(solution)/shard_map/ppermute | solution.py:710
  1403.7 45.4 %collective-permute-start.31 = (bf16[96,6144]{1,0:T(8,128)(2,1)S(1)}, bf16[96,6144]{1,0:T(8,128)(2,1)S(1)}, u32[]{:S(2)}, u32[]{:S(2)}) collective-permute-start(bf16[96,6144]{1,0:T(8,128)(2,1)S(1)} %bitcast.676), channel_id=1, source_target_pairs={{0,1},{1,0},{2,3},{3,2},{4,5},{5,4},{6,7},{7,6},{8,9},{9,8},{10,11... | collective-permute-start | bytes 3538952 | tf_op jit(solution)/shard_map/ppermute | solution.py:701
  1449.7 14.3 collective-permute-start.35
  (264 other events, 3246.7 us)
Sparse Core Ops, SparseCore 0:
  1077.7 68.5 all-gather.1
